TPU v7x, 512 devices: a whole 4x4x16 slice. The times are simulated.
512 devices in a mesh: blk: 128 (over x_lo, y, z), grp: 4 (over x_hi, core).
Axes of the slice: x: 4 (x_hi: 2, x_lo: 2; x = x_hi * 2 + x_lo), y: 4, z: 16, core: 2. Of those that a mesh axis runs over, the one named last changes fastest.
Arguments:
- tables: float32 [8, 131072, 128], P('grp', 'blk'), may hold values from -1 to 1
- bag_ids: int32 [16384, 8, 32], P('blk', 'grp'), may hold values from 0 to 8191, as said below
Outputs:
- pooled: float32 [16384, 8, 128], P('blk', 'grp')
- interaction: float32 [16384, 8, 8], P('blk', 'grp')
Inputs may be any that keep to these rules, and one draw needn't show every extreme that they name: `bag_ids`: some rows are far more popular than others.
All inputs are finite; a program needn't handle non-finite values.
Results may differ from a plain program's by a relative error of at most 0.000065.
Values sent between devices are 32-bit elements; how exact they have to be, the bound alone decides.
No kernel may reach another device: no remote copies, remote signals or barrier semaphores. Data moves between devices by JAX's collectives and lax.ppermute only.
A program may use at most 64 MiB of HBM per device.

v0:
```python
import jax
import jax.numpy as jnp
from jax import lax
from jax.sharding import PartitionSpec as P

SECTIONS = 8


def from_behind(value, axis, steps):
    count = lax.axis_size(axis)
    pairs = [(source, (source + steps) % count) for source in range(count)]
    return lax.ppermute(value, axis, pairs)


def pool_shard(table_rows, bag_codes, offset):
    samples = bag_codes.shape[0]
    shard_rows = table_rows.shape[1]
    inside = (bag_codes % SECTIONS == offset).astype(jnp.float32)
    local_row = bag_codes // SECTIONS
    sample_index = jnp.arange(samples, dtype=jnp.int32)[:, None]
    results = []
    for table_num in range(table_rows.shape[0]):
        counts = jnp.zeros((samples, shard_rows), jnp.float32)
        counts = counts.at[sample_index, local_row[:, table_num, :]].add(inside[:, table_num, :])
        results.append(
            jnp.dot(
                counts,
                table_rows[table_num],
                precision=lax.Precision.HIGHEST,
                preferred_element_type=jnp.float32,
            )
        )
    return jnp.stack(results, axis=1)


def shards(tables, bag_ids):
    pooled = pool_shard(tables, bag_ids, 0)
    for offset in range(1, SECTIONS):
        arrived = from_behind(bag_ids, "blk", -offset)
        partial_value = pool_shard(tables, arrived, offset)
        pooled = pooled + from_behind(partial_value, "blk", offset)
    gathered = lax.all_gather(pooled, "grp", axis=1, tiled=True)
    interaction = (
        jnp.einsum("bte,bue->btu", pooled, gathered, precision=lax.Precision.HIGHEST)
        / pooled.shape[2]
    )
    return (pooled, interaction)


def solution(mesh):
    return jax.shard_map(
        shards,
        mesh=mesh,
        in_specs=(P("grp", "blk", None), P("blk", "grp", None)),
        out_specs=(P("blk", "grp", None), P("blk", "grp", None)),
        check_vma=False,
    )
```

profile of v0, /device:TPU:1, one launch (start us, length us, event | category | flops | bytes accessed | tf_op | source)
XLA Modules:
  0.0 603.1 jit_solution(1696953147470570175)
XLA Ops:
  0.6 16.2 %collective-permute-start.4 = (s32[128,2,32]{0,2,1:T(8,128)}, s32[128,2,32]{0,2,1:T(8,128)S(1)}, u32[]{:S(2)}, u32[]{:S(2)}) collective-permute-start(s32[128,2,32]{0,2,1:T(8,128)} %param.3), channel_id=1, source_target_pairs={{0,500},{4,504},{8,508},{12,0},{16,4},{20,8},{24,12},{28,16},{32,2... | collective-permute-start | bytes 98312 | tf_op jit(solution)/shard_map/ppermute | solution.py:12
  16.9 4.3 collective-permute-start.2
  23.8 2.8 collective-permute-start.8
  29.8 11.6 %collective-permute-start.12 = (s32[128,2,32]{0,2,1:T(8,128)S(1)}, s32[128,2,32]{0,2,1:T(8,128)S(1)}, u32[]{:S(2)}, u32[]{:S(2)}) collective-permute-start(s32[128,2,32]{0,2,1:T(8,128)S(1)} %copy-done.3), channel_id=1, source_target_pairs={{0,484},{4,488},{8,492},{12,496},{16,500},{20,504},{24,508},{28,0}... | collective-permute-start | bytes 98312 | tf_op jit(solution)/shard_map/ppermute | solution.py:12
  41.5 2.8 collective-permute-start.10
  44.8 7.1 %collective-permute-done.10 = s32[128,2,32]{0,2,1:T(8,128)S(1)} collective-permute-done((s32[128,2,32]{0,2,1:T(8,128)S(1)}, s32[128,2,32]{0,2,1:T(8,128)S(1)}, u32[]{:S(2)}, u32[]{:S(2)}) %collective-permute-start.10) | collective-permute-done | bytes 32800 | tf_op jit(solution)/shard_map/ppermute | solution.py:12
  59.5 28.4 %scatter_custom_fusion = f32[131072]{0:T(1024)S(1)} fusion(s32[4096]{0:T(1024)S(1)} %reshape.518, f32[4096]{0:T(1024)S(1)} %reshape.520, f32[]{:T(128)} %constant.122.clone.1), kind=kCustom, calls=%fused_computation.96 | custom fusion | flops 4096 | bytes 524292
  88.0 28.4 %scatter_custom_fusion.2 = f32[131072]{0:T(1024)S(1)} fusion(s32[4096]{0:T(1024)S(1)} %reshape.530, f32[4096]{0:T(1024)S(1)} %reshape.532, f32[]{:T(128)} %constant.122.clone.1), kind=kCustom, calls=%fused_computation.92 | custom fusion | flops 4096 | bytes 524292
  117.8 28.4 %scatter_custom_fusion.4 = f32[131072]{0:T(1024)S(1)} fusion(s32[4096]{0:T(1024)S(1)} %reshape.542, f32[4096]{0:T(1024)S(1)} %reshape.544, f32[]{:T(128)} %constant.122.clone.1), kind=kCustom, calls=%fused_computation.88 | custom fusion | flops 4096 | bytes 524292
  147.0 28.6 %scatter_custom_fusion.6 = f32[131072]{0:T(1024)S(1)} fusion(s32[4096]{0:T(1024)S(1)} %reshape.554, f32[4096]{0:T(1024)S(1)} %reshape.556, f32[]{:T(128)} %constant.122.clone.1), kind=kCustom, calls=%fused_computation.84 | custom fusion | flops 4096 | bytes 524292
  176.3 28.4 %scatter_custom_fusion.8 = f32[131072]{0:T(1024)S(1)} fusion(s32[4096]{0:T(1024)S(1)} %reshape.566, f32[4096]{0:T(1024)S(1)} %reshape.568, f32[]{:T(128)} %constant.122.clone.1), kind=kCustom, calls=%fused_computation.80 | custom fusion | flops 4096 | bytes 524292
  205.5 28.4 %scatter_custom_fusion.14 = f32[131072]{0:T(1024)S(1)} fusion(s32[4096]{0:T(1024)S(1)} %reshape.602, f32[4096]{0:T(1024)S(1)} %reshape.604, f32[]{:T(128)} %constant.122.clone.1), kind=kCustom, calls=%fused_computation.68 | custom fusion | flops 4096 | bytes 524292
  234.6 28.4 %scatter_custom_fusion.12 = f32[131072]{0:T(1024)S(1)} fusion(s32[4096]{0:T(1024)S(1)} %reshape.590, f32[4096]{0:T(1024)S(1)} %reshape.592, f32[]{:T(128)} %constant.122.clone.1), kind=kCustom, calls=%fused_computation.72 | custom fusion | flops 4096 | bytes 524292
  263.8 28.4 %scatter_custom_fusion.10 = f32[131072]{0:T(1024)S(1)} fusion(s32[4096]{0:T(1024)S(1)} %reshape.578, f32[4096]{0:T(1024)S(1)} %reshape.580, f32[]{:T(128)} %constant.122.clone.1), kind=kCustom, calls=%fused_computation.76 | custom fusion | flops 4096 | bytes 524292
  293.0 28.4 %scatter_custom_fusion.3 = f32[131072]{0:T(1024)S(1)} fusion(s32[4096]{0:T(1024)S(1)} %reshape.536, f32[4096]{0:T(1024)S(1)} %reshape.538, f32[]{:T(128)} %constant.122.clone.1), kind=kCustom, calls=%fused_computation.90 | custom fusion | flops 4096 | bytes 524292
  322.2 2.6 collective-permute-start.1
  324.8 28.6 %scatter_custom_fusion.5 = f32[131072]{0:T(1024)S(1)} fusion(s32[4096]{0:T(1024)S(1)} %reshape.548, f32[4096]{0:T(1024)S(1)} %reshape.550, f32[]{:T(128)} %constant.122.clone.1), kind=kCustom, calls=%fused_computation.86 | custom fusion | flops 4096 | bytes 524292
  354.2 3.3 collective-permute-start.3
  357.5 28.4 %scatter_custom_fusion.7 = f32[131072]{0:T(1024)S(1)} fusion(s32[4096]{0:T(1024)S(1)} %reshape.560, f32[4096]{0:T(1024)S(1)} %reshape.562, f32[]{:T(128)} %constant.122.clone.1), kind=kCustom, calls=%fused_computation.82 | custom fusion | flops 4096 | bytes 524292
  386.7 4.2 collective-permute-start.5
  390.9 28.4 %scatter_custom_fusion.9 = f32[131072]{0:T(1024)S(1)} fusion(s32[4096]{0:T(1024)S(1)} %reshape.572, f32[4096]{0:T(1024)S(1)} %reshape.574, f32[]{:T(128)} %constant.122.clone.1), kind=kCustom, calls=%fused_computation.78 | custom fusion | flops 4096 | bytes 524292
  420.7 5.8 collective-permute-start.7
  426.5 28.4 %scatter_custom_fusion.15 = f32[131072]{0:T(1024)S(1)} fusion(s32[4096]{0:T(1024)S(1)} %reshape.608, f32[4096]{0:T(1024)S(1)} %reshape.610, f32[]{:T(128)} %constant.122.clone.1), kind=kCustom, calls=%fused_computation.66 | custom fusion | flops 4096 | bytes 524292
  456.3 5.8 collective-permute-start.13
  462.2 28.6 %scatter_custom_fusion.13 = f32[131072]{0:T(1024)S(1)} fusion(s32[4096]{0:T(1024)} %reshape.596, f32[4096]{0:T(1024)S(1)} %reshape.598, f32[]{:T(128)} %constant.122.clone.1), kind=kCustom, calls=%fused_computation.70 | custom fusion | flops 4096 | bytes 524800
  491.5 28.7 %scatter_custom_fusion.11 = f32[131072]{0:T(1024)S(1)} fusion(s32[4096]{0:T(1024)S(1)} %reshape.584, f32[4096]{0:T(1024)S(1)} %reshape.586, f32[]{:T(128)} %constant.122.clone.1), kind=kCustom, calls=%fused_computation.74 | custom fusion | flops 4096 | bytes 524292
  521.7 28.4 %scatter_custom_fusion.1 = f32[131072]{0:T(1024)S(1)} fusion(s32[4096]{0:T(1024)S(1)} %reshape.524, f32[4096]{0:T(1024)S(1)} %reshape.526, f32[]{:T(128)} %constant.122.clone.1), kind=kCustom, calls=%fused_computation.94 | custom fusion | flops 4096 | bytes 524292
  551.2 4.1 collective-permute-start.11
  555.2 4.2 collective-permute-start.9
  560.1 10.1 %collective-permute-done.11 = f32[128,2,128]{2,0,1:T(8,128)S(1)} collective-permute-done((f32[128,2,128]{2,0,1:T(8,128)S(1)}, f32[128,2,128]{2,0,1:T(8,128)S(1)}, u32[]{:S(2)}, u32[]{:S(2)}) %collective-permute-start.11) | collective-permute-done | bytes 131104 | tf_op jit(solution)/shard_map/ppermute | solution.py:12
  570.2 12.9 %collective-permute-done.9 = f32[128,2,128]{2,0,1:T(8,128)S(1)} collective-permute-done((f32[128,2,128]{2,0,1:T(8,128)S(1)}, f32[128,2,128]{2,0,1:T(8,128)S(1)}, u32[]{:S(2)}, u32[]{:S(2)}) %collective-permute-start.9) | collective-permute-done | bytes 131104 | tf_op jit(solution)/shard_map/ppermute | solution.py:12
  583.3 17.5 %all_gather.3 = f32[128,8,128]{2,0,1:T(8,128)S(1)} all-gather(f32[128,2,128]{2,0,1:T(8,128)S(1)} %fusion.70), channel_id=1, replica_groups=mesh['blk'=128,'grp'=4] {'grp'}, dimensions={1}, use_global_device_ids=true | all-gather | bytes 655360 | tf_op jit(solution)/shard_map/all_gather | solution.py:42
  (175 shorter events, 30.1 us)
Async XLA Ops:
  0.6 28.7 %copy-start.3 = (s32[128,2,32]{0,2,1:T(8,128)S(1)}, s32[128,2,32]{0,2,1:T(8,128)}, u32[]{:S(2)}) copy-start(s32[128,2,32]{0,2,1:T(8,128)} %param.3) | copy-start | bytes 98308
  0.6 29.1 %collective-permute-start.4 = (s32[128,2,32]{0,2,1:T(8,128)}, s32[128,2,32]{0,2,1:T(8,128)S(1)}, u32[]{:S(2)}, u32[]{:S(2)}) collective-permute-start(s32[128,2,32]{0,2,1:T(8,128)} %param.3), channel_id=1, source_target_pairs={{0,500},{4,504},{8,508},{12,0},{16,4},{20,8},{24,12},{28,16},{32,2... | collective-permute-start | bytes 98312 | tf_op jit(solution)/shard_map/ppermute | solution.py:12
  16.9 24.7 %collective-permute-start.2 = (s32[128,2,32]{0,2,1:T(8,128)}, s32[128,2,32]{0,2,1:T(8,128)S(1)}, u32[]{:S(2)}, u32[]{:S(2)}) collective-permute-start(s32[128,2,32]{0,2,1:T(8,128)} %param.3), channel_id=1, source_target_pairs={{0,504},{4,508},{8,0},{12,4},{16,8},{20,12},{24,16},{28,20},{32,24... | collective-permute-start | bytes 98312 | tf_op jit(solution)/shard_map/ppermute | solution.py:12
  21.2 23.3 %collective-permute-start = (s32[128,2,32]{0,2,1:T(8,128)}, s32[128,2,32]{0,2,1:T(8,128)S(1)}, u32[]{:S(2)}, u32[]{:S(2)}) collective-permute-start(s32[128,2,32]{0,2,1:T(8,128)} %param.3), channel_id=1, source_target_pairs={{0,508},{4,0},{8,4},{12,8},{16,12},{20,16},{24,20},{28,24},{32,28}... | collective-permute-start | bytes 98312 | tf_op jit(solution)/shard_map/ppermute | solution.py:12
  23.8 20.7 %collective-permute-start.8 = (s32[128,2,32]{0,2,1:T(8,128)}, s32[128,2,32]{0,2,1:T(8,128)S(1)}, u32[]{:S(2)}, u32[]{:S(2)}) collective-permute-start(s32[128,2,32]{0,2,1:T(8,128)} %param.3), channel_id=1, source_target_pairs={{0,492},{4,496},{8,500},{12,504},{16,508},{20,0},{24,4},{28,8},{32... | collective-permute-start | bytes 98312 | tf_op jit(solution)/shard_map/ppermute | solution.py:12
  26.6 18.0 %collective-permute-start.6 = (s32[128,2,32]{0,2,1:T(8,128)}, s32[128,2,32]{0,2,1:T(8,128)S(1)}, u32[]{:S(2)}, u32[]{:S(2)}) collective-permute-start(s32[128,2,32]{0,2,1:T(8,128)} %param.3), channel_id=1, source_target_pairs={{0,496},{4,500},{8,504},{12,508},{16,0},{20,4},{24,8},{28,12},{32,... | collective-permute-start | bytes 98312 | tf_op jit(solution)/shard_map/ppermute | solution.py:12
  29.8 14.9 %collective-permute-start.12 = (s32[128,2,32]{0,2,1:T(8,128)S(1)}, s32[128,2,32]{0,2,1:T(8,128)S(1)}, u32[]{:S(2)}, u32[]{:S(2)}) collective-permute-start(s32[128,2,32]{0,2,1:T(8,128)S(1)} %copy-done.3), channel_id=1, source_target_pairs={{0,484},{4,488},{8,492},{12,496},{16,500},{20,504},{24,508},{28,0}... | collective-permute-start | bytes 98312 | tf_op jit(solution)/shard_map/ppermute | solution.py:12
  41.5 10.4 %collective-permute-start.10 = (s32[128,2,32]{0,2,1:T(8,128)S(1)}, s32[128,2,32]{0,2,1:T(8,128)S(1)}, u32[]{:S(2)}, u32[]{:S(2)}) collective-permute-start(s32[128,2,32]{0,2,1:T(8,128)S(1)} %copy-done.3), channel_id=1, source_target_pairs={{0,488},{4,492},{8,496},{12,500},{16,504},{20,508},{24,0},{28,4},{... | collective-permute-start | bytes 98312 | tf_op jit(solution)/shard_map/ppermute | solution.py:12
  54.6 0.7 copy-start.5
  55.3 0.7 copy-start.4
  88.0 28.5 %copy-start = (f32[2,1024,128]{2,1,0:T(8,128)S(1)}, f32[2,1024,128]{2,1,0:T(8,128)}, u32[]{:S(2)}) copy-start(f32[2,1024,128]{2,1,0:T(8,128)} %param.2) | copy-start | bytes 3145732
  322.2 228.1 %collective-permute-start.1 = (f32[128,2,128]{2,0,1:T(8,128)S(1)}, f32[128,2,128]{2,0,1:T(8,128)S(1)}, u32[]{:S(2)}, u32[]{:S(2)}) collective-permute-start(f32[128,2,128]{2,0,1:T(8,128)S(1)} %pad_maximum_fusion), channel_id=1, source_target_pairs={{0,4},{4,8},{8,12},{12,16},{16,20},{20,24},{24,28},{28,32},{32,36}... | collective-permute-start | bytes 393224 | tf_op jit(solution)/shard_map/ppermute | solution.py:12
  354.2 201.0 %collective-permute-start.3 = (f32[128,2,128]{2,0,1:T(8,128)S(1)}, f32[128,2,128]{2,0,1:T(8,128)S(1)}, u32[]{:S(2)}, u32[]{:S(2)}) collective-permute-start(f32[128,2,128]{2,0,1:T(8,128)S(1)} %pad_maximum_fusion.1), channel_id=1, source_target_pairs={{0,8},{4,12},{8,16},{12,20},{16,24},{20,28},{24,32},{28,36},{32,40... | collective-permute-start | bytes 393224 | tf_op jit(solution)/shard_map/ppermute | solution.py:12
  386.7 173.4 %collective-permute-start.5 = (f32[128,2,128]{2,0,1:T(8,128)S(1)}, f32[128,2,128]{2,0,1:T(8,128)S(1)}, u32[]{:S(2)}, u32[]{:S(2)}) collective-permute-start(f32[128,2,128]{2,0,1:T(8,128)S(1)} %pad_maximum_fusion.2), channel_id=1, source_target_pairs={{0,12},{4,16},{8,20},{12,24},{16,28},{20,32},{24,36},{28,40},{32,4... | collective-permute-start | bytes 393224 | tf_op jit(solution)/shard_map/ppermute | solution.py:12
  420.7 139.4 %collective-permute-start.7 = (f32[128,2,128]{2,0,1:T(8,128)}, f32[128,2,128]{2,0,1:T(8,128)S(1)}, u32[]{:S(2)}, u32[]{:S(2)}) collective-permute-start(f32[128,2,128]{2,0,1:T(8,128)} %pad_maximum_fusion.3), channel_id=1, source_target_pairs={{0,16},{4,20},{8,24},{12,28},{16,32},{20,36},{24,40},{28,44},{32,4... | collective-permute-start | bytes 393224 | tf_op jit(solution)/shard_map/ppermute | solution.py:12
  456.3 103.8 %collective-permute-start.13 = (f32[128,2,128]{2,0,1:T(8,128)}, f32[128,2,128]{2,0,1:T(8,128)S(1)}, u32[]{:S(2)}, u32[]{:S(2)}) collective-permute-start(f32[128,2,128]{2,0,1:T(8,128)} %pad_maximum_fusion.6), channel_id=1, source_target_pairs={{0,28},{4,32},{8,36},{12,40},{16,44},{20,48},{24,52},{28,56},{32,6... | collective-permute-start | bytes 393224 | tf_op jit(solution)/shard_map/ppermute | solution.py:12
  550.3 0.9 copy-start.2
  551.2 19.1 %collective-permute-start.11 = (f32[128,2,128]{2,0,1:T(8,128)S(1)}, f32[128,2,128]{2,0,1:T(8,128)S(1)}, u32[]{:S(2)}, u32[]{:S(2)}) collective-permute-start(f32[128,2,128]{2,0,1:T(8,128)S(1)} %copy-done.2), channel_id=1, source_target_pairs={{0,24},{4,28},{8,32},{12,36},{16,40},{20,44},{24,48},{28,52},{32,5... | collective-permute-start | bytes 393224 | tf_op jit(solution)/shard_map/ppermute | solution.py:12
  555.2 27.8 %collective-permute-start.9 = (f32[128,2,128]{2,0,1:T(8,128)S(1)}, f32[128,2,128]{2,0,1:T(8,128)S(1)}, u32[]{:S(2)}, u32[]{:S(2)}) collective-permute-start(f32[128,2,128]{2,0,1:T(8,128)S(1)} %pad_maximum_fusion.4), channel_id=1, source_target_pairs={{0,20},{4,24},{8,28},{12,32},{16,36},{20,40},{24,44},{28,48},{32,5... | collective-permute-start | bytes 393224 | tf_op jit(solution)/shard_map/ppermute | solution.py:12
  583.2 17.5 %copy-start.1 = (f32[128,2,128]{2,1,0:T(2,128)}, f32[128,2,128]{2,1,0:T(2,128)S(1)}, u32[]{:S(2)}) copy-start(f32[128,2,128]{2,1,0:T(2,128)S(1)} %copy.62) | copy-start | bytes 393220
where the time goes:
time: 612 us; the launch traced here: 603 us
  other arithmetic  459 us (75%)
  starting transfers between devices  72.3 us (12%)
  waiting for transfers between devices  30.1 us (5%)
  blocking collectives  17.5 us (3%)
  matrix products  11.4 us (2%)
  local copies, waits for them, and re-layouts  10.5 us (2%)
    unnamed x26, other arithmetic  456 us
    ppermute x14, starting transfers between devices, from_behind(): return lax.ppermute(value, axis, pairs)  72.3 us
    ppermute x14, waiting for transfers between devices, from_behind(): return lax.ppermute(value, axis, pairs)  30.1 us
    all_gather x1, blocking collectives, shards(): gathered = lax.all_gather(pooled, 'grp', axis=1, tiled=True)  17.5 us
  transfers between devices with their start and end apart: 14, of which 3 were waited for; matrix products, arithmetic and copies ran while one was open for 35% of the time, Pallas kernels for 0%

commit v1 on v0

v1 whole, which is shorter than its diff:
```python
import jax
import jax.numpy as jnp
from jax import lax
from jax.experimental import pallas as pl
from jax.experimental.pallas import tpu as pltpu
from jax.sharding import PartitionSpec as P

SECTIONS = 8
VMEM_LIMIT = 8 * 1024 * 1024


def shift(value, axis, steps):
    count = lax.axis_size(axis)
    pairs = [(source, (source + steps) % count) for source in range(count)]
    return lax.ppermute(value, axis, pairs)


def vmem(count):
    return [pl.BlockSpec(memory_space=pltpu.VMEM)] * count


def prepare(tables):
    count, rows, width = tables.shape

    def kernel(table_ref, out_ref):
        for table_num in range(count):
            for start in range(0, rows, 256):
                part = table_ref[table_num, start : start + 256, :].T
                high = part.astype(jnp.bfloat16)
                low = (part - high.astype(jnp.float32)).astype(jnp.bfloat16)
                out_ref[table_num, :width, start : start + 256] = high
                out_ref[table_num, width:, start : start + 256] = low

    return pl.pallas_call(
        kernel,
        out_shape=jax.ShapeDtypeStruct((count, 2 * width, rows), jnp.bfloat16),
        in_specs=vmem(1),
        out_specs=vmem(1)[0],
        cost_estimate=pl.CostEstimate(flops=4_000_000, bytes_accessed=2_000_000, transcendentals=0),
        compiler_params=pltpu.CompilerParams(vmem_limit_bytes=VMEM_LIMIT),
        name="prepare",
    )(tables)


def add_counts(codes, offset, count_ref, slots, chunk):
    samples = codes.shape[1]
    row = lax.shift_right_logical(codes, 3)
    slot = row & (slots - 1)
    lane = lax.shift_right_logical(row, 8) * 8
    unit = jnp.where((codes & (SECTIONS - 1)) == offset, jnp.left_shift(1, lane), 0)
    for start in range(0, slots, chunk):
        place = lax.broadcasted_iota(jnp.int32, (chunk, samples), 0) + start
        total = jnp.zeros((chunk, samples), jnp.int32)
        for entry in range(codes.shape[0]):
            total = total + jnp.where(
                place == slot[entry : entry + 1, :], unit[entry : entry + 1, :], 0
            )
        for quarter in range(4):
            piece = lax.shift_right_logical(total, 8 * quarter) & 255
            at = quarter * slots + start
            count_ref[at : at + chunk, :] = piece.astype(jnp.float32).astype(jnp.bfloat16)


def visit(split, state, offset, fresh, keep):
    tables, twice, rows = split.shape
    width = twice // 2
    samples = state.shape[1]
    head = tables * width
    base = 0 if fresh else head
    entries = state.shape[0] - base
    bag = entries // tables

    def kernel(split_ref, state_ref, out_ref, count_ref):
        for table_num in range(tables):
            first = base + table_num * bag
            codes = state_ref[first : first + bag, :].astype(jnp.int32)
            add_counts(codes, offset, count_ref.at[table_num], rows // 4, 128)
            both = jnp.dot(
                split_ref[table_num], count_ref[table_num], preferred_element_type=jnp.float32
            )
            value = both[:width] + both[width:]
            at = table_num * width
            if not fresh:
                value = value + state_ref[at : at + width, :]
            out_ref[at : at + width, :] = value
        if keep:
            out_ref[head:, :] = state_ref[base:, :]

    return pl.pallas_call(
        kernel,
        out_shape=jax.ShapeDtypeStruct((head + (entries if keep else 0), samples), jnp.float32),
        in_specs=vmem(2),
        out_specs=vmem(1)[0],
        scratch_shapes=[pltpu.VMEM((tables, rows, samples), jnp.bfloat16)],
        cost_estimate=pl.CostEstimate(flops=140_000_000, bytes_accessed=1_300_000, transcendentals=0),
        compiler_params=pltpu.CompilerParams(vmem_limit_bytes=VMEM_LIMIT),
        name="visit%d" % offset,
    )(split, state)


def join(one, two, tables):
    height, samples = one.shape
    width = height // tables

    def kernel(one_ref, two_ref, sum_ref, out_ref):
        for table_num in range(tables):
            at = table_num * width
            value = one_ref[at : at + width, :] + two_ref[at : at + width, :]
            sum_ref[at : at + width, :] = value
            out_ref[:, table_num, :] = value.T

    return pl.pallas_call(
        kernel,
        out_shape=(
            jax.ShapeDtypeStruct((height, samples), jnp.float32),
            jax.ShapeDtypeStruct((samples, tables, width), jnp.float32),
        ),
        in_specs=vmem(2),
        out_specs=tuple(vmem(2)),
        cost_estimate=pl.CostEstimate(flops=4_000_000, bytes_accessed=500_000, transcendentals=0),
        compiler_params=pltpu.CompilerParams(vmem_limit_bytes=VMEM_LIMIT),
        name="join",
    )(one, two)


def interact(pooled, gathered, width):
    samples = pooled.shape[1]
    tables = pooled.shape[0] // width
    others = gathered.shape[0] // width

    def kernel(pooled_ref, gathered_ref, inter_ref):
        rows = []
        for table_num in range(tables):
            own = pooled_ref[table_num * width : (table_num + 1) * width, :]
            for other in range(others):
                there = gathered_ref[other * width : (other + 1) * width, :]
                rows.append(jnp.sum(own * there, axis=0, keepdims=True))
        inter_ref[...] = jnp.concatenate(rows, axis=0) / width

    return pl.pallas_call(
        kernel,
        out_shape=jax.ShapeDtypeStruct((tables * others, samples), jnp.float32),
        in_specs=vmem(2),
        out_specs=vmem(1)[0],
        cost_estimate=pl.CostEstimate(flops=4_000_000, bytes_accessed=700_000, transcendentals=0),
        compiler_params=pltpu.CompilerParams(vmem_limit_bytes=VMEM_LIMIT),
        name="interact",
    )(pooled, gathered)


def shards(tables, bag_ids):
    samples, count, bag = bag_ids.shape
    width = tables.shape[2]
    ids = bag_ids.reshape(samples, count * bag).T.astype(jnp.float32)
    far = shift(ids, "blk", -7)
    split = prepare(tables)
    back = visit(split, ids, 0, True, True)
    back = shift(back, "blk", -1)
    ahead = visit(split, far, 7, True, True)
    ahead = shift(ahead, "blk", 1)
    back = shift(visit(split, back, 1, False, True), "blk", -1)
    ahead = shift(visit(split, ahead, 6, False, True), "blk", 1)
    back = shift(visit(split, back, 2, False, True), "blk", -1)
    ahead = shift(visit(split, ahead, 5, False, True), "blk", 1)
    back = shift(visit(split, back, 3, False, False), "blk", -1)
    ahead = visit(split, ahead, 4, False, False)
    pooled, result = join(ahead, back, count)
    result = shift(result, "blk", 4)
    gathered = lax.all_gather(pooled, "grp", axis=0, tiled=True)
    inter = shift(interact(pooled, gathered, width), "blk", 4)
    return result, inter.reshape(count, -1, samples).transpose(2, 0, 1)


def solution(mesh):
    return jax.shard_map(
        shards,
        mesh=mesh,
        in_specs=(P("grp", "blk", None), P("blk", "grp", None)),
        out_specs=(P("blk", "grp", None), P("blk", "grp", None)),
        check_vma=False,
    )
```

time: 612 us -> 98.4 us (0.16); the launches traced: 603 us -> 97.9 us
  other arithmetic: 459 us -> 0.01 us
  starting transfers between devices: 72.3 us -> 54.2 us
  waiting for transfers between devices: 30.1 us -> 14.7 us
  Pallas kernels: 0 us -> 12.9 us
  matrix products: 11.4 us -> 0 us
  local copies, waits for them, and re-layouts: 10.5 us -> 2.89 us
    unnamed x26 -> x0, other arithmetic: 456 us -> none
    ppermute x14 -> x10, starting transfers between devices: 72.3 us -> 54.2 us  [shift(): return lax.ppermute(value, axis, pairs)]
    ppermute x14 -> x10, waiting for transfers between devices: 30.1 us -> 14.7 us  [shift(): return lax.ppermute(value, axis, pairs)]
    pallas_call x0 -> x11, Pallas kernels: none -> 12.9 us  [the longest x8 12.3 us: visit(): pl.pallas_call(kernel, out_shape=jax.ShapeDtypeStruct((head + (entries if...]
    dot_general x17 -> x0, matrix products: 11.4 us -> none  [the longest x16 10.2 us: pool_shard(): jnp.dot(counts, table_rows[table_num], precision=lax.Precision.HIGHEST, p...]
  transfers between devices with their start and end apart: 14 -> 10, of which waited for: 3 -> 3; matrix products, arithmetic and copies ran while one was open for 35% -> 0% of each run, Pallas kernels for 0% -> 11%
where the time goes in v1:
time: 98.4 us; the launch traced here: 97.9 us
  starting transfers between devices  54.2 us (55%)
  waiting for transfers between devices  14.7 us (15%)
  Pallas kernels  12.9 us (13%)
  blocking collectives  12.5 us (13%)
  local copies, waits for them, and re-layouts  2.89 us (3%)
    ppermute x10, starting transfers between devices, shift(): return lax.ppermute(value, axis, pairs)  54.2 us
    ppermute x10, waiting for transfers between devices, shift(): return lax.ppermute(value, axis, pairs)  14.7 us
    all_gather x1, blocking collectives, shards(): gathered = lax.all_gather(pooled, 'grp', axis=0, tiled=True)  12.5 us
    pallas_call x8, Pallas kernels, visit(): pl.pallas_call(kernel, out_shape=jax.ShapeDtypeStruct((head + (entries if...  12.3 us
    unnamed x6, local copies, waits for them, and re-layouts  2.89 us
  transfers between devices with their start and end apart: 10, of which 3 were waited for; matrix products, arithmetic and copies ran while one was open for 0% of the time, Pallas kernels for 11%

profile of v1, /device:TPU:1, one launch (start us, length us, event | category | flops | bytes accessed | tf_op | source)
XLA Modules:
  0.0 97.9 jit_solution(2220296322127272228)
XLA Ops:
  0.6 1.2 %copy-done = f32[2,1024,128]{2,1,0:T(8,128)S(1)} copy-done((f32[2,1024,128]{2,1,0:T(8,128)S(1)}, f32[2,1024,128]{2,1,0:T(8,128)}, u32[]{:S(2)}) %copy-start) | copy-done | bytes 1048600
  1.9 0.3 prepare.1.split_ref
  2.2 0.4 copy-done.1
  2.6 1.5 %visit0.1 = f32[320,128]{1,0:T(8,128)S(1)} custom-call(bf16[2,256,1024]{2,1,0:T(8,128)(2,1)S(1)} %prepare.1.split_ref, f32[64,128]{1,0:T(8,128)S(1)} %bitcast.6), custom_call_target="tpu_custom_call" | custom-call | flops 140000000 | bytes 1300000 | tf_op jit(solution)/shard_map/visit0/pallas_call | solution.py:89
  4.2 15.3 %collective-permute-start.4 = (f32[320,128]{1,0:T(8,128)S(1)}, f32[320,128]{1,0:T(8,128)S(1)}, u32[]{:S(2)}, u32[]{:S(2)}) collective-permute-start(f32[320,128]{1,0:T(8,128)S(1)} %visit0.1), channel_id=1, source_target_pairs={{0,508},{4,0},{8,4},{12,8},{16,12},{20,16},{24,20},{28,24},{32,28}... | collective-permute-start | bytes 491528 | tf_op jit(solution)/shard_map/ppermute | solution.py:15
  19.5 6.5 %collective-permute-start = (f32[64,128]{1,0:T(8,128)S(1)}, f32[64,128]{1,0:T(8,128)S(1)}, u32[]{:S(2)}, u32[]{:S(2)}) collective-permute-start(f32[64,128]{1,0:T(8,128)S(1)} %bitcast.7), channel_id=1, source_target_pairs={{0,484},{4,488},{8,492},{12,496},{16,500},{20,504},{24,508},{28,0}... | collective-permute-start | bytes 98312 | tf_op jit(solution)/shard_map/ppermute | solution.py:15
  26.0 4.9 %collective-permute-done.state_ref = f32[64,128]{1,0:T(8,128)S(1)} collective-permute-done((f32[64,128]{1,0:T(8,128)S(1)}, f32[64,128]{1,0:T(8,128)S(1)}, u32[]{:S(2)}, u32[]{:S(2)}) %collective-permute-start) | collective-permute-done | bytes 32800 | tf_op jit(solution)/shard_map/ppermute | solution.py:15
  30.9 1.5 %visit7.1 = f32[320,128]{1,0:T(8,128)S(1)} custom-call(bf16[2,256,1024]{2,1,0:T(8,128)(2,1)S(1)} %prepare.1.split_ref, f32[64,128]{1,0:T(8,128)S(1)} %collective-permute-done.state_ref), custom_call_target="tpu_custom_call" | custom-call | flops 140000000 | bytes 1300000 | tf_op jit(solution)/shard_map/visit7/pallas_call | solution.py:89
  32.4 1.9 %collective-permute-start.1 = (f32[320,128]{1,0:T(8,128)S(1)}, f32[320,128]{1,0:T(8,128)S(1)}, u32[]{:S(2)}, u32[]{:S(2)}) collective-permute-start(f32[320,128]{1,0:T(8,128)S(1)} %visit7.1), channel_id=1, source_target_pairs={{0,4},{4,8},{8,12},{12,16},{16,20},{20,24},{24,28},{28,32},{32,36}... | collective-permute-start | bytes 491528 | tf_op jit(solution)/shard_map/ppermute | solution.py:15
  34.4 0.0 collective-permute-done.4.state_ref
  34.4 1.5 %visit1.1 = f32[320,128]{1,0:T(8,128)S(1)} custom-call(bf16[2,256,1024]{2,1,0:T(8,128)(2,1)S(1)} %prepare.1.split_ref, f32[320,128]{1,0:T(8,128)S(1)} %collective-permute-done.4.state_ref), custom_call_target="tpu_custom_call" | custom-call | flops 140000000 | bytes 1300000 | tf_op jit(solution)/shard_map/visit1/pallas_call | solution.py:89
  35.9 7.6 %collective-permute-start.5 = (f32[320,128]{1,0:T(8,128)S(1)}, f32[320,128]{1,0:T(8,128)S(1)}, u32[]{:S(2)}, u32[]{:S(2)}) collective-permute-start(f32[320,128]{1,0:T(8,128)S(1)} %visit1.1), channel_id=1, source_target_pairs={{0,508},{4,0},{8,4},{12,8},{16,12},{20,16},{24,20},{28,24},{32,28}... | collective-permute-start | bytes 491528 | tf_op jit(solution)/shard_map/ppermute | solution.py:15
  43.5 0.0 collective-permute-done.1.state_ref
  43.5 1.5 %visit6.1 = f32[320,128]{1,0:T(8,128)S(1)} custom-call(bf16[2,256,1024]{2,1,0:T(8,128)(2,1)S(1)} %prepare.1.split_ref, f32[320,128]{1,0:T(8,128)S(1)} %collective-permute-done.1.state_ref), custom_call_target="tpu_custom_call" | custom-call | flops 140000000 | bytes 1300000 | tf_op jit(solution)/shard_map/visit6/pallas_call | solution.py:89
  45.1 1.9 %collective-permute-start.2 = (f32[320,128]{1,0:T(8,128)S(1)}, f32[320,128]{1,0:T(8,128)S(1)}, u32[]{:S(2)}, u32[]{:S(2)}) collective-permute-start(f32[320,128]{1,0:T(8,128)S(1)} %visit6.1), channel_id=1, source_target_pairs={{0,4},{4,8},{8,12},{12,16},{16,20},{20,24},{24,28},{28,32},{32,36}... | collective-permute-start | bytes 491528 | tf_op jit(solution)/shard_map/ppermute | solution.py:15
  47.0 0.0 collective-permute-done.5.state_ref
  47.0 1.5 %visit2.1 = f32[320,128]{1,0:T(8,128)S(1)} custom-call(bf16[2,256,1024]{2,1,0:T(8,128)(2,1)S(1)} %prepare.1.split_ref, f32[320,128]{1,0:T(8,128)S(1)} %collective-permute-done.5.state_ref), custom_call_target="tpu_custom_call" | custom-call | flops 140000000 | bytes 1300000 | tf_op jit(solution)/shard_map/visit2/pallas_call | solution.py:89
  48.5 7.6 %collective-permute-start.6 = (f32[320,128]{1,0:T(8,128)S(1)}, f32[320,128]{1,0:T(8,128)S(1)}, u32[]{:S(2)}, u32[]{:S(2)}) collective-permute-start(f32[320,128]{1,0:T(8,128)S(1)} %visit2.1), channel_id=1, source_target_pairs={{0,508},{4,0},{8,4},{12,8},{16,12},{20,16},{24,20},{28,24},{32,28}... | collective-permute-start | bytes 491528 | tf_op jit(solution)/shard_map/ppermute | solution.py:15
  56.1 1.5 %visit5.1 = f32[320,128]{1,0:T(8,128)S(1)} custom-call(bf16[2,256,1024]{2,1,0:T(8,128)(2,1)S(1)} %prepare.1.split_ref, f32[320,128]{1,0:T(8,128)S(1)} %collective-permute-done.2.state_ref), custom_call_target="tpu_custom_call" | custom-call | flops 140000000 | bytes 1300000 | tf_op jit(solution)/shard_map/visit5/pallas_call | solution.py:89
  57.7 1.9 %collective-permute-start.3 = (f32[320,128]{1,0:T(8,128)S(1)}, f32[320,128]{1,0:T(8,128)S(1)}, u32[]{:S(2)}, u32[]{:S(2)}) collective-permute-start(f32[320,128]{1,0:T(8,128)S(1)} %visit5.1), channel_id=1, source_target_pairs={{0,4},{4,8},{8,12},{12,16},{16,20},{20,24},{24,28},{28,32},{32,36}... | collective-permute-start | bytes 491528 | tf_op jit(solution)/shard_map/ppermute | solution.py:15
  59.6 1.5 %visit3.1 = f32[256,128]{1,0:T(8,128)S(1)} custom-call(bf16[2,256,1024]{2,1,0:T(8,128)(2,1)S(1)} %prepare.1.split_ref, f32[320,128]{1,0:T(8,128)S(1)} %collective-permute-done.6.state_ref), custom_call_target="tpu_custom_call" | custom-call | flops 140000000 | bytes 1300000 | tf_op jit(solution)/shard_map/visit3/pallas_call | solution.py:89
  61.2 7.6 %collective-permute-start.7 = (f32[256,128]{1,0:T(8,128)S(1)}, f32[256,128]{1,0:T(8,128)S(1)}, u32[]{:S(2)}, u32[]{:S(2)}) collective-permute-start(f32[256,128]{1,0:T(8,128)S(1)} %visit3.1), channel_id=1, source_target_pairs={{0,508},{4,0},{8,4},{12,8},{16,12},{20,16},{24,20},{28,24},{32,28}... | collective-permute-start | bytes 393224 | tf_op jit(solution)/shard_map/ppermute | solution.py:15
  68.8 1.5 %visit4.1.one_ref = f32[256,128]{1,0:T(8,128)S(1)} custom-call(bf16[2,256,1024]{2,1,0:T(8,128)(2,1)S(1)} %prepare.1.split_ref, f32[320,128]{1,0:T(8,128)S(1)} %collective-permute-done.3.state_ref), custom_call_target="tpu_custom_call" | custom-call | flops 140000000 | bytes 1300000 | tf_op jit(solution)/shard_map/visit4/pallas_call | solution.py:89
  70.3 0.4 collective-permute-done.7.two_ref
  70.7 0.1 join.1
  70.8 1.9 %collective-permute-start.8 = (f32[128,2,128]{2,1,0:T(2,128)S(1)}, f32[128,2,128]{2,1,0:T(2,128)S(1)}, u32[]{:S(2)}, u32[]{:S(2)}) collective-permute-start(f32[128,2,128]{2,1,0:T(2,128)S(1)} %get-tuple-element.4), channel_id=1, source_target_pairs={{0,16},{4,20},{8,24},{12,28},{16,32},{20,36},{24,40},{28,44},{32,4... | collective-permute-start | bytes 393224 | tf_op jit(solution)/shard_map/ppermute | solution.py:15
  72.8 12.5 %all_gather.3.gathered_ref = f32[1024,128]{1,0:T(8,128)S(1)} all-gather(f32[256,128]{1,0:T(8,128)S(1)} %get-tuple-element.5.pooled_ref), channel_id=1, replica_groups=mesh['blk'=128,'grp'=4] {'grp'}, dimensions={0}, use_global_device_ids=true | all-gather | bytes 655360 | tf_op jit(solution)/shard_map/all_gather | solution.py:169
  85.2 0.1 interact.1
  85.3 1.9 %collective-permute-start.9 = (f32[16,128]{1,0:T(8,128)S(1)}, f32[16,128]{1,0:T(8,128)S(1)}, u32[]{:S(2)}, u32[]{:S(2)}) collective-permute-start(f32[16,128]{1,0:T(8,128)S(1)} %interact.1), channel_id=1, source_target_pairs={{0,16},{4,20},{8,24},{12,28},{16,32},{20,36},{24,40},{28,44},{32,4... | collective-permute-start | bytes 24584 | tf_op jit(solution)/shard_map/ppermute | solution.py:15
  87.3 9.4 %collective-permute-done.9 = f32[16,128]{1,0:T(8,128)S(1)} collective-permute-done((f32[16,128]{1,0:T(8,128)S(1)}, f32[16,128]{1,0:T(8,128)S(1)}, u32[]{:S(2)}, u32[]{:S(2)}) %collective-permute-start.9) | collective-permute-done | bytes 8224 | tf_op jit(solution)/shard_map/ppermute | solution.py:15
  96.7 0.7 copy.6
  97.3 0.6 copy.7
  (7 shorter events, 0.0 us)
Async XLA Ops:
  0.6 1.2 %copy-start = (f32[2,1024,128]{2,1,0:T(8,128)S(1)}, f32[2,1024,128]{2,1,0:T(8,128)}, u32[]{:S(2)}) copy-start(f32[2,1024,128]{2,1,0:T(8,128)} %table_ref.1) | copy-start | bytes 3145732
  1.9 0.8 copy-start.1
  4.2 30.2 %collective-permute-start.4 = (f32[320,128]{1,0:T(8,128)S(1)}, f32[320,128]{1,0:T(8,128)S(1)}, u32[]{:S(2)}, u32[]{:S(2)}) collective-permute-start(f32[320,128]{1,0:T(8,128)S(1)} %visit0.1), channel_id=1, source_target_pairs={{0,508},{4,0},{8,4},{12,8},{16,12},{20,16},{24,20},{28,24},{32,28}... | collective-permute-start | bytes 491528 | tf_op jit(solution)/shard_map/ppermute | solution.py:15
  19.5 11.4 %collective-permute-start = (f32[64,128]{1,0:T(8,128)S(1)}, f32[64,128]{1,0:T(8,128)S(1)}, u32[]{:S(2)}, u32[]{:S(2)}) collective-permute-start(f32[64,128]{1,0:T(8,128)S(1)} %bitcast.7), channel_id=1, source_target_pairs={{0,484},{4,488},{8,492},{12,496},{16,500},{20,504},{24,508},{28,0}... | collective-permute-start | bytes 98312 | tf_op jit(solution)/shard_map/ppermute | solution.py:15
  32.4 11.1 %collective-permute-start.1 = (f32[320,128]{1,0:T(8,128)S(1)}, f32[320,128]{1,0:T(8,128)S(1)}, u32[]{:S(2)}, u32[]{:S(2)}) collective-permute-start(f32[320,128]{1,0:T(8,128)S(1)} %visit7.1), channel_id=1, source_target_pairs={{0,4},{4,8},{8,12},{12,16},{16,20},{20,24},{24,28},{28,32},{32,36}... | collective-permute-start | bytes 491528 | tf_op jit(solution)/shard_map/ppermute | solution.py:15
  35.9 11.1 %collective-permute-start.5 = (f32[320,128]{1,0:T(8,128)S(1)}, f32[320,128]{1,0:T(8,128)S(1)}, u32[]{:S(2)}, u32[]{:S(2)}) collective-permute-start(f32[320,128]{1,0:T(8,128)S(1)} %visit1.1), channel_id=1, source_target_pairs={{0,508},{4,0},{8,4},{12,8},{16,12},{20,16},{24,20},{28,24},{32,28}... | collective-permute-start | bytes 491528 | tf_op jit(solution)/shard_map/ppermute | solution.py:15
  45.1 11.1 %collective-permute-start.2 = (f32[320,128]{1,0:T(8,128)S(1)}, f32[320,128]{1,0:T(8,128)S(1)}, u32[]{:S(2)}, u32[]{:S(2)}) collective-permute-start(f32[320,128]{1,0:T(8,128)S(1)} %visit6.1), channel_id=1, source_target_pairs={{0,4},{4,8},{8,12},{12,16},{16,20},{20,24},{24,28},{28,32},{32,36}... | collective-permute-start | bytes 491528 | tf_op jit(solution)/shard_map/ppermute | solution.py:15
  48.5 11.1 %collective-permute-start.6 = (f32[320,128]{1,0:T(8,128)S(1)}, f32[320,128]{1,0:T(8,128)S(1)}, u32[]{:S(2)}, u32[]{:S(2)}) collective-permute-start(f32[320,128]{1,0:T(8,128)S(1)} %visit2.1), channel_id=1, source_target_pairs={{0,508},{4,0},{8,4},{12,8},{16,12},{20,16},{24,20},{28,24},{32,28}... | collective-permute-start | bytes 491528 | tf_op jit(solution)/shard_map/ppermute | solution.py:15
  57.7 11.1 %collective-permute-start.3 = (f32[320,128]{1,0:T(8,128)S(1)}, f32[320,128]{1,0:T(8,128)S(1)}, u32[]{:S(2)}, u32[]{:S(2)}) collective-permute-start(f32[320,128]{1,0:T(8,128)S(1)} %visit5.1), channel_id=1, source_target_pairs={{0,4},{4,8},{8,12},{12,16},{16,20},{20,24},{24,28},{28,32},{32,36}... | collective-permute-start | bytes 491528 | tf_op jit(solution)/shard_map/ppermute | solution.py:15
  61.2 9.5 %collective-permute-start.7 = (f32[256,128]{1,0:T(8,128)S(1)}, f32[256,128]{1,0:T(8,128)S(1)}, u32[]{:S(2)}, u32[]{:S(2)}) collective-permute-start(f32[256,128]{1,0:T(8,128)S(1)} %visit3.1), channel_id=1, source_target_pairs={{0,508},{4,0},{8,4},{12,8},{16,12},{20,16},{24,20},{28,24},{32,28}... | collective-permute-start | bytes 393224 | tf_op jit(solution)/shard_map/ppermute | solution.py:15
  70.8 25.8 %collective-permute-start.8 = (f32[128,2,128]{2,1,0:T(2,128)S(1)}, f32[128,2,128]{2,1,0:T(2,128)S(1)}, u32[]{:S(2)}, u32[]{:S(2)}) collective-permute-start(f32[128,2,128]{2,1,0:T(2,128)S(1)} %get-tuple-element.4), channel_id=1, source_target_pairs={{0,16},{4,20},{8,24},{12,28},{16,32},{20,36},{24,40},{28,44},{32,4... | collective-permute-start | bytes 393224 | tf_op jit(solution)/shard_map/ppermute | solution.py:15
  85.3 11.3 %collective-permute-start.9 = (f32[16,128]{1,0:T(8,128)S(1)}, f32[16,128]{1,0:T(8,128)S(1)}, u32[]{:S(2)}, u32[]{:S(2)}) collective-permute-start(f32[16,128]{1,0:T(8,128)S(1)} %interact.1), channel_id=1, source_target_pairs={{0,16},{4,20},{8,24},{12,28},{16,32},{20,36},{24,40},{28,44},{32,4... | collective-permute-start | bytes 24584 | tf_op jit(solution)/shard_map/ppermute | solution.py:15

commit v2 on v1

--- a/solution.py
+++ b/solution.py
@@ -4,6 +4,7 @@
 from jax.experimental import pallas as pl
 from jax.experimental.pallas import tpu as pltpu
 from jax.sharding import PartitionSpec as P
+
 
 SECTIONS = 8
 VMEM_LIMIT = 8 * 1024 * 1024
@@ -42,23 +43,33 @@
     )(tables)
 
 
-def add_counts(codes, offset, count_ref, slots, chunk):
-    samples = codes.shape[1]
+def add_counts(codes, offset, count_ref):
+    rows, samples = count_ref.shape
+    slots = rows // 8
+    entries = codes.shape[0]
     row = lax.shift_right_logical(codes, 3)
     slot = row & (slots - 1)
-    lane = lax.shift_right_logical(row, 8) * 8
-    unit = jnp.where((codes & (SECTIONS - 1)) == offset, jnp.left_shift(1, lane), 0)
-    for start in range(0, slots, chunk):
-        place = lax.broadcasted_iota(jnp.int32, (chunk, samples), 0) + start
-        total = jnp.zeros((chunk, samples), jnp.int32)
-        for entry in range(codes.shape[0]):
-            total = total + jnp.where(
-                place == slot[entry : entry + 1, :], unit[entry : entry + 1, :], 0
-            )
-        for quarter in range(4):
-            piece = lax.shift_right_logical(total, 8 * quarter) & 255
-            at = quarter * slots + start
-            count_ref[at : at + chunk, :] = piece.astype(jnp.float32).astype(jnp.bfloat16)
+    place4 = lax.shift_right_logical(row, slots.bit_length() - 1) * 4
+    unit = jnp.where((codes & (SECTIONS - 1)) == offset, jnp.left_shift(1, place4), 0)
+    mask = 0x0F0F0F0F
+    for start in range(0, slots, 64):
+        place = lax.broadcasted_iota(jnp.int32, (64, samples), 0) + start
+        even = odd = None
+        for first in range(0, entries, 11):
+            total = jnp.zeros((64, samples), jnp.int32)
+            for entry in range(first, min(first + 11, entries)):
+                total = total + jnp.where(
+                    place == slot[entry : entry + 1, :], unit[entry : entry + 1, :], 0
+                )
+            low = total & mask
+            high = lax.shift_right_logical(total, 4) & mask
+            even = low if even is None else even + low
+            odd = high if odd is None else odd + high
+        for pair in range(4):
+            for half, word in enumerate((even, odd)):
+                piece = lax.shift_right_logical(word, 8 * pair) & 255
+                at = (2 * pair + half) * slots + start
+                count_ref[at : at + 64, :] = piece.astype(jnp.float32).astype(jnp.bfloat16)
 
 
 def visit(split, state, offset, fresh, keep):
@@ -74,7 +85,7 @@
         for table_num in range(tables):
             first = base + table_num * bag
             codes = state_ref[first : first + bag, :].astype(jnp.int32)
-            add_counts(codes, offset, count_ref.at[table_num], rows // 4, 128)
+            add_counts(codes, offset, count_ref.at[table_num])
             both = jnp.dot(
                 split_ref[table_num], count_ref[table_num], preferred_element_type=jnp.float32
             )
@@ -84,7 +95,7 @@
                 value = value + state_ref[at : at + width, :]
             out_ref[at : at + width, :] = value
         if keep:
-            out_ref[head:, :] = state_ref[base:, :]
+            out_ref[head:, :] = state_ref[base:, :].astype(jnp.float32)
 
     return pl.pallas_call(
         kernel,
@@ -94,7 +105,6 @@
         scratch_shapes=[pltpu.VMEM((tables, rows, samples), jnp.bfloat16)],
         cost_estimate=pl.CostEstimate(flops=140_000_000, bytes_accessed=1_300_000, transcendentals=0),
         compiler_params=pltpu.CompilerParams(vmem_limit_bytes=VMEM_LIMIT),
-        name="visit%d" % offset,
     )(split, state)
 
 
@@ -151,7 +161,7 @@
 def shards(tables, bag_ids):
     samples, count, bag = bag_ids.shape
     width = tables.shape[2]
-    ids = bag_ids.reshape(samples, count * bag).T.astype(jnp.float32)
+    ids = bag_ids.reshape(samples, count * bag).T
     far = shift(ids, "blk", -7)
     split = prepare(tables)
     back = visit(split, ids, 0, True, True)
@@ -167,7 +177,8 @@
     pooled, result = join(ahead, back, count)
     result = shift(result, "blk", 4)
     gathered = lax.all_gather(pooled, "grp", axis=0, tiled=True)
-    inter = shift(interact(pooled, gathered, width), "blk", 4)
+    inter = interact(pooled, gathered, width)
+    inter = shift(inter, "blk", 4)
     return result, inter.reshape(count, -1, samples).transpose(2, 0, 1)
 
 

time: 98.4 us -> 95.6 us (0.972)
  Pallas kernels: 12.9 us -> 8.85 us
    pallas_call x8, Pallas kernels: 12.3 us -> 8.26 us  [visit(): pl.pallas_call(kernel, out_shape=jax.ShapeDtypeStruct((head + (entries if...]
  transfers between devices with their start and end apart: 10 -> 10, of which waited for: 3 -> 3; matrix products, arithmetic and copies ran while one was open for 0% -> 0% of each run, Pallas kernels for 11% -> 8%
where the time goes in v2:
time: 95.6 us; the launch traced here: 95 us
  starting transfers between devices  54.2 us (57%)
  waiting for transfers between devices  15.2 us (16%)
  blocking collectives  13.1 us (14%)
  Pallas kernels  8.85 us (9%)
  local copies, waits for them, and re-layouts  2.89 us (3%)
    ppermute x10, starting transfers between devices, shift(): return lax.ppermute(value, axis, pairs)  54.2 us
    ppermute x10, waiting for transfers between devices, shift(): return lax.ppermute(value, axis, pairs)  15.2 us
    all_gather x1, blocking collectives, shards(): gathered = lax.all_gather(pooled, 'grp', axis=0, tiled=True)  13.1 us
    pallas_call x8, Pallas kernels, visit(): pl.pallas_call(kernel, out_shape=jax.ShapeDtypeStruct((head + (entries if...  8.26 us
    unnamed x6, local copies, waits for them, and re-layouts  2.89 us
  transfers between devices with their start and end apart: 10, of which 3 were waited for; matrix products, arithmetic and copies ran while one was open for 0% of the time, Pallas kernels for 8%

profile of v2, /device:TPU:1, one launch (start us, length us, event | category | flops | bytes accessed | tf_op | source)
XLA Modules:
  0.0 95.0 jit_solution(8522014981612276276)
XLA Ops:
  0.6 1.2 %copy-done = f32[2,1024,128]{2,1,0:T(8,128)S(1)} copy-done((f32[2,1024,128]{2,1,0:T(8,128)S(1)}, f32[2,1024,128]{2,1,0:T(8,128)}, u32[]{:S(2)}) %copy-start) | copy-done | bytes 1048600
  1.9 0.3 prepare.1.split_ref
  2.2 0.4 copy-done.1
  2.6 1.0 %shard_map.45 = f32[320,128]{1,0:T(8,128)S(1)} custom-call(bf16[2,256,1024]{2,1,0:T(8,128)(2,1)S(1)} %prepare.1.split_ref, s32[64,128]{1,0:T(8,128)S(1)} %bitcast.6), custom_call_target="tpu_custom_call" | custom-call | flops 140000000 | bytes 1300000 | tf_op jit(solution)/shard_map/pallas_call | solution.py:100
  3.7 15.3 %collective-permute-start.4 = (f32[320,128]{1,0:T(8,128)S(1)}, f32[320,128]{1,0:T(8,128)S(1)}, u32[]{:S(2)}, u32[]{:S(2)}) collective-permute-start(f32[320,128]{1,0:T(8,128)S(1)} %shard_map.45), channel_id=1, source_target_pairs={{0,508},{4,0},{8,4},{12,8},{16,12},{20,16},{24,20},{28,24},{32,28}... | collective-permute-start | bytes 491528 | tf_op jit(solution)/shard_map/ppermute | solution.py:16
  19.0 6.5 %collective-permute-start = (s32[64,128]{1,0:T(8,128)S(1)}, s32[64,128]{1,0:T(8,128)S(1)}, u32[]{:S(2)}, u32[]{:S(2)}) collective-permute-start(s32[64,128]{1,0:T(8,128)S(1)} %bitcast.7), channel_id=1, source_target_pairs={{0,484},{4,488},{8,492},{12,496},{16,500},{20,504},{24,508},{28,0}... | collective-permute-start | bytes 98312 | tf_op jit(solution)/shard_map/ppermute | solution.py:16
  25.5 4.9 %collective-permute-done.state_ref = s32[64,128]{1,0:T(8,128)S(1)} collective-permute-done((s32[64,128]{1,0:T(8,128)S(1)}, s32[64,128]{1,0:T(8,128)S(1)}, u32[]{:S(2)}, u32[]{:S(2)}) %collective-permute-start) | collective-permute-done | bytes 32800 | tf_op jit(solution)/shard_map/ppermute | solution.py:16
  30.4 1.0 %shard_map.41 = f32[320,128]{1,0:T(8,128)S(1)} custom-call(bf16[2,256,1024]{2,1,0:T(8,128)(2,1)S(1)} %prepare.1.split_ref, s32[64,128]{1,0:T(8,128)S(1)} %collective-permute-done.state_ref), custom_call_target="tpu_custom_call" | custom-call | flops 140000000 | bytes 1300000 | tf_op jit(solution)/shard_map/pallas_call | solution.py:100
  31.4 1.9 %collective-permute-start.1 = (f32[320,128]{1,0:T(8,128)S(1)}, f32[320,128]{1,0:T(8,128)S(1)}, u32[]{:S(2)}, u32[]{:S(2)}) collective-permute-start(f32[320,128]{1,0:T(8,128)S(1)} %shard_map.41), channel_id=1, source_target_pairs={{0,4},{4,8},{8,12},{12,16},{16,20},{20,24},{24,28},{28,32},{32,36}... | collective-permute-start | bytes 491528 | tf_op jit(solution)/shard_map/ppermute | solution.py:16
  33.4 0.0 collective-permute-done.4.state_ref
  33.4 1.0 %shard_map.46 = f32[320,128]{1,0:T(8,128)S(1)} custom-call(bf16[2,256,1024]{2,1,0:T(8,128)(2,1)S(1)} %prepare.1.split_ref, f32[320,128]{1,0:T(8,128)S(1)} %collective-permute-done.4.state_ref), custom_call_target="tpu_custom_call" | custom-call | flops 140000000 | bytes 1300000 | tf_op jit(solution)/shard_map/pallas_call | solution.py:100
  34.4 7.6 %collective-permute-start.5 = (f32[320,128]{1,0:T(8,128)S(1)}, f32[320,128]{1,0:T(8,128)S(1)}, u32[]{:S(2)}, u32[]{:S(2)}) collective-permute-start(f32[320,128]{1,0:T(8,128)S(1)} %shard_map.46), channel_id=1, source_target_pairs={{0,508},{4,0},{8,4},{12,8},{16,12},{20,16},{24,20},{28,24},{32,28}... | collective-permute-start | bytes 491528 | tf_op jit(solution)/shard_map/ppermute | solution.py:16
  42.0 0.0 collective-permute-done.1.state_ref
  42.0 1.0 %shard_map.42 = f32[320,128]{1,0:T(8,128)S(1)} custom-call(bf16[2,256,1024]{2,1,0:T(8,128)(2,1)S(1)} %prepare.1.split_ref, f32[320,128]{1,0:T(8,128)S(1)} %collective-permute-done.1.state_ref), custom_call_target="tpu_custom_call" | custom-call | flops 140000000 | bytes 1300000 | tf_op jit(solution)/shard_map/pallas_call | solution.py:100
  43.0 1.9 %collective-permute-start.2 = (f32[320,128]{1,0:T(8,128)S(1)}, f32[320,128]{1,0:T(8,128)S(1)}, u32[]{:S(2)}, u32[]{:S(2)}) collective-permute-start(f32[320,128]{1,0:T(8,128)S(1)} %shard_map.42), channel_id=1, source_target_pairs={{0,4},{4,8},{8,12},{12,16},{16,20},{20,24},{24,28},{28,32},{32,36}... | collective-permute-start | bytes 491528 | tf_op jit(solution)/shard_map/ppermute | solution.py:16
  45.0 0.0 collective-permute-done.5.state_ref
  45.0 1.0 %shard_map.47 = f32[320,128]{1,0:T(8,128)S(1)} custom-call(bf16[2,256,1024]{2,1,0:T(8,128)(2,1)S(1)} %prepare.1.split_ref, f32[320,128]{1,0:T(8,128)S(1)} %collective-permute-done.5.state_ref), custom_call_target="tpu_custom_call" | custom-call | flops 140000000 | bytes 1300000 | tf_op jit(solution)/shard_map/pallas_call | solution.py:100
  46.0 7.6 %collective-permute-start.6 = (f32[320,128]{1,0:T(8,128)S(1)}, f32[320,128]{1,0:T(8,128)S(1)}, u32[]{:S(2)}, u32[]{:S(2)}) collective-permute-start(f32[320,128]{1,0:T(8,128)S(1)} %shard_map.47), channel_id=1, source_target_pairs={{0,508},{4,0},{8,4},{12,8},{16,12},{20,16},{24,20},{28,24},{32,28}... | collective-permute-start | bytes 491528 | tf_op jit(solution)/shard_map/ppermute | solution.py:16
  53.6 1.0 %shard_map.43 = f32[320,128]{1,0:T(8,128)S(1)} custom-call(bf16[2,256,1024]{2,1,0:T(8,128)(2,1)S(1)} %prepare.1.split_ref, f32[320,128]{1,0:T(8,128)S(1)} %collective-permute-done.2.state_ref), custom_call_target="tpu_custom_call" | custom-call | flops 140000000 | bytes 1300000 | tf_op jit(solution)/shard_map/pallas_call | solution.py:100
  54.7 1.9 %collective-permute-start.3 = (f32[320,128]{1,0:T(8,128)S(1)}, f32[320,128]{1,0:T(8,128)S(1)}, u32[]{:S(2)}, u32[]{:S(2)}) collective-permute-start(f32[320,128]{1,0:T(8,128)S(1)} %shard_map.43), channel_id=1, source_target_pairs={{0,4},{4,8},{8,12},{12,16},{16,20},{20,24},{24,28},{28,32},{32,36}... | collective-permute-start | bytes 491528 | tf_op jit(solution)/shard_map/ppermute | solution.py:16
  56.6 1.0 %shard_map.48 = f32[256,128]{1,0:T(8,128)S(1)} custom-call(bf16[2,256,1024]{2,1,0:T(8,128)(2,1)S(1)} %prepare.1.split_ref, f32[320,128]{1,0:T(8,128)S(1)} %collective-permute-done.6.state_ref), custom_call_target="tpu_custom_call" | custom-call | flops 140000000 | bytes 1300000 | tf_op jit(solution)/shard_map/pallas_call | solution.py:100
  57.6 7.6 %collective-permute-start.7 = (f32[256,128]{1,0:T(8,128)S(1)}, f32[256,128]{1,0:T(8,128)S(1)}, u32[]{:S(2)}, u32[]{:S(2)}) collective-permute-start(f32[256,128]{1,0:T(8,128)S(1)} %shard_map.48), channel_id=1, source_target_pairs={{0,508},{4,0},{8,4},{12,8},{16,12},{20,16},{24,20},{28,24},{32,28}... | collective-permute-start | bytes 393224 | tf_op jit(solution)/shard_map/ppermute | solution.py:16
  65.2 1.0 %shard_map.44.one_ref = f32[256,128]{1,0:T(8,128)S(1)} custom-call(bf16[2,256,1024]{2,1,0:T(8,128)(2,1)S(1)} %prepare.1.split_ref, f32[320,128]{1,0:T(8,128)S(1)} %collective-permute-done.3.state_ref), custom_call_target="tpu_custom_call" | custom-call | flops 140000000 | bytes 1300000 | tf_op jit(solution)/shard_map/pallas_call | solution.py:100
  66.3 0.9 collective-permute-done.7.two_ref
  67.1 0.1 join.1
  67.3 1.9 %collective-permute-start.8 = (f32[128,2,128]{2,1,0:T(2,128)S(1)}, f32[128,2,128]{2,1,0:T(2,128)S(1)}, u32[]{:S(2)}, u32[]{:S(2)}) collective-permute-start(f32[128,2,128]{2,1,0:T(2,128)S(1)} %get-tuple-element.4), channel_id=1, source_target_pairs={{0,16},{4,20},{8,24},{12,28},{16,32},{20,36},{24,40},{28,44},{32,4... | collective-permute-start | bytes 393224 | tf_op jit(solution)/shard_map/ppermute | solution.py:16
  69.2 13.1 %all_gather.3.gathered_ref = f32[1024,128]{1,0:T(8,128)S(1)} all-gather(f32[256,128]{1,0:T(8,128)S(1)} %get-tuple-element.5.pooled_ref), channel_id=1, replica_groups=mesh['blk'=128,'grp'=4] {'grp'}, dimensions={0}, use_global_device_ids=true | all-gather | bytes 655360 | tf_op jit(solution)/shard_map/all_gather | solution.py:179
  82.3 0.1 interact.1
  82.4 1.9 %collective-permute-start.9 = (f32[16,128]{1,0:T(8,128)S(1)}, f32[16,128]{1,0:T(8,128)S(1)}, u32[]{:S(2)}, u32[]{:S(2)}) collective-permute-start(f32[16,128]{1,0:T(8,128)S(1)} %interact.1), channel_id=1, source_target_pairs={{0,16},{4,20},{8,24},{12,28},{16,32},{20,36},{24,40},{28,44},{32,4... | collective-permute-start | bytes 24584 | tf_op jit(solution)/shard_map/ppermute | solution.py:16
  84.3 9.4 %collective-permute-done.9 = f32[16,128]{1,0:T(8,128)S(1)} collective-permute-done((f32[16,128]{1,0:T(8,128)S(1)}, f32[16,128]{1,0:T(8,128)S(1)}, u32[]{:S(2)}, u32[]{:S(2)}) %collective-permute-start.9) | collective-permute-done | bytes 8224 | tf_op jit(solution)/shard_map/ppermute | solution.py:16
  93.7 0.7 copy.6
  94.4 0.6 copy.7
  (6 shorter events, 0.0 us)
Async XLA Ops:
  0.6 1.2 %copy-start = (f32[2,1024,128]{2,1,0:T(8,128)S(1)}, f32[2,1024,128]{2,1,0:T(8,128)}, u32[]{:S(2)}) copy-start(f32[2,1024,128]{2,1,0:T(8,128)} %table_ref.1) | copy-start | bytes 3145732
  1.9 0.8 copy-start.1
  3.7 29.7 %collective-permute-start.4 = (f32[320,128]{1,0:T(8,128)S(1)}, f32[320,128]{1,0:T(8,128)S(1)}, u32[]{:S(2)}, u32[]{:S(2)}) collective-permute-start(f32[320,128]{1,0:T(8,128)S(1)} %shard_map.45), channel_id=1, source_target_pairs={{0,508},{4,0},{8,4},{12,8},{16,12},{20,16},{24,20},{28,24},{32,28}... | collective-permute-start | bytes 491528 | tf_op jit(solution)/shard_map/ppermute | solution.py:16
  19.0 11.4 %collective-permute-start = (s32[64,128]{1,0:T(8,128)S(1)}, s32[64,128]{1,0:T(8,128)S(1)}, u32[]{:S(2)}, u32[]{:S(2)}) collective-permute-start(s32[64,128]{1,0:T(8,128)S(1)} %bitcast.7), channel_id=1, source_target_pairs={{0,484},{4,488},{8,492},{12,496},{16,500},{20,504},{24,508},{28,0}... | collective-permute-start | bytes 98312 | tf_op jit(solution)/shard_map/ppermute | solution.py:16
  31.4 10.6 %collective-permute-start.1 = (f32[320,128]{1,0:T(8,128)S(1)}, f32[320,128]{1,0:T(8,128)S(1)}, u32[]{:S(2)}, u32[]{:S(2)}) collective-permute-start(f32[320,128]{1,0:T(8,128)S(1)} %shard_map.41), channel_id=1, source_target_pairs={{0,4},{4,8},{8,12},{12,16},{16,20},{20,24},{24,28},{28,32},{32,36}... | collective-permute-start | bytes 491528 | tf_op jit(solution)/shard_map/ppermute | solution.py:16
  34.4 10.6 %collective-permute-start.5 = (f32[320,128]{1,0:T(8,128)S(1)}, f32[320,128]{1,0:T(8,128)S(1)}, u32[]{:S(2)}, u32[]{:S(2)}) collective-permute-start(f32[320,128]{1,0:T(8,128)S(1)} %shard_map.46), channel_id=1, source_target_pairs={{0,508},{4,0},{8,4},{12,8},{16,12},{20,16},{24,20},{28,24},{32,28}... | collective-permute-start | bytes 491528 | tf_op jit(solution)/shard_map/ppermute | solution.py:16
  43.0 10.6 %collective-permute-start.2 = (f32[320,128]{1,0:T(8,128)S(1)}, f32[320,128]{1,0:T(8,128)S(1)}, u32[]{:S(2)}, u32[]{:S(2)}) collective-permute-start(f32[320,128]{1,0:T(8,128)S(1)} %shard_map.42), channel_id=1, source_target_pairs={{0,4},{4,8},{8,12},{12,16},{16,20},{20,24},{24,28},{28,32},{32,36}... | collective-permute-start | bytes 491528 | tf_op jit(solution)/shard_map/ppermute | solution.py:16
  46.0 10.6 %collective-permute-start.6 = (f32[320,128]{1,0:T(8,128)S(1)}, f32[320,128]{1,0:T(8,128)S(1)}, u32[]{:S(2)}, u32[]{:S(2)}) collective-permute-start(f32[320,128]{1,0:T(8,128)S(1)} %shard_map.47), channel_id=1, source_target_pairs={{0,508},{4,0},{8,4},{12,8},{16,12},{20,16},{24,20},{28,24},{32,28}... | collective-permute-start | bytes 491528 | tf_op jit(solution)/shard_map/ppermute | solution.py:16
  54.7 10.6 %collective-permute-start.3 = (f32[320,128]{1,0:T(8,128)S(1)}, f32[320,128]{1,0:T(8,128)S(1)}, u32[]{:S(2)}, u32[]{:S(2)}) collective-permute-start(f32[320,128]{1,0:T(8,128)S(1)} %shard_map.43), channel_id=1, source_target_pairs={{0,4},{4,8},{8,12},{12,16},{16,20},{20,24},{24,28},{28,32},{32,36}... | collective-permute-start | bytes 491528 | tf_op jit(solution)/shard_map/ppermute | solution.py:16
  57.6 9.5 %collective-permute-start.7 = (f32[256,128]{1,0:T(8,128)S(1)}, f32[256,128]{1,0:T(8,128)S(1)}, u32[]{:S(2)}, u32[]{:S(2)}) collective-permute-start(f32[256,128]{1,0:T(8,128)S(1)} %shard_map.48), channel_id=1, source_target_pairs={{0,508},{4,0},{8,4},{12,8},{16,12},{20,16},{24,20},{28,24},{32,28}... | collective-permute-start | bytes 393224 | tf_op jit(solution)/shard_map/ppermute | solution.py:16
  67.3 26.4 %collective-permute-start.8 = (f32[128,2,128]{2,1,0:T(2,128)S(1)}, f32[128,2,128]{2,1,0:T(2,128)S(1)}, u32[]{:S(2)}, u32[]{:S(2)}) collective-permute-start(f32[128,2,128]{2,1,0:T(2,128)S(1)} %get-tuple-element.4), channel_id=1, source_target_pairs={{0,16},{4,20},{8,24},{12,28},{16,32},{20,36},{24,40},{28,44},{32,4... | collective-permute-start | bytes 393224 | tf_op jit(solution)/shard_map/ppermute | solution.py:16
  82.4 11.3 %collective-permute-start.9 = (f32[16,128]{1,0:T(8,128)S(1)}, f32[16,128]{1,0:T(8,128)S(1)}, u32[]{:S(2)}, u32[]{:S(2)}) collective-permute-start(f32[16,128]{1,0:T(8,128)S(1)} %interact.1), channel_id=1, source_target_pairs={{0,16},{4,20},{8,24},{12,28},{16,32},{20,36},{24,40},{28,44},{32,4... | collective-permute-start | bytes 24584 | tf_op jit(solution)/shard_map/ppermute | solution.py:16

commit v3 on v2

--- a/solution.py
+++ b/solution.py
@@ -43,37 +43,64 @@
     )(tables)
 
 
-def add_counts(codes, offset, count_ref):
-    rows, samples = count_ref.shape
-    slots = rows // 8
+def count_rows(codes, offset, first_row, height):
+    samples = codes.shape[1]
     entries = codes.shape[0]
-    row = lax.shift_right_logical(codes, 3)
-    slot = row & (slots - 1)
-    place4 = lax.shift_right_logical(row, slots.bit_length() - 1) * 4
-    unit = jnp.where((codes & (SECTIONS - 1)) == offset, jnp.left_shift(1, place4), 0)
-    mask = 0x0F0F0F0F
-    for start in range(0, slots, 64):
-        place = lax.broadcasted_iota(jnp.int32, (64, samples), 0) + start
-        even = odd = None
-        for first in range(0, entries, 11):
-            total = jnp.zeros((64, samples), jnp.int32)
-            for entry in range(first, min(first + 11, entries)):
-                total = total + jnp.where(
+    slots = height // 16
+    row = lax.shift_right_logical(codes, 3) - first_row
+    hit = ((codes & (SECTIONS - 1)) == offset) & (row >= 0) & (row < height)
+    slot = jnp.where(hit, row & (slots - 1), -1)
+    unit = jnp.left_shift(1, lax.shift_right_logical(row, slots.bit_length() - 1) * 2 & 31)
+    place = lax.broadcasted_iota(jnp.int32, (slots, samples), 0)
+
+    def plus(total, more):
+        return more if total is None else [x + y for x, y in zip(total, more)]
+
+    def split(word, bits, mask):
+        return [word & mask, lax.shift_right_logical(word, bits) & mask]
+
+    eight = None
+    for first in range(0, entries, 15):
+        four = None
+        for start in range(first, min(first + 15, entries), 3):
+            two = None
+            for entry in range(start, min(start + 3, entries)):
+                one = jnp.where(
                     place == slot[entry : entry + 1, :], unit[entry : entry + 1, :], 0
                 )
-            low = total & mask
-            high = lax.shift_right_logical(total, 4) & mask
-            even = low if even is None else even + low
-            odd = high if odd is None else odd + high
-        for pair in range(4):
-            for half, word in enumerate((even, odd)):
-                piece = lax.shift_right_logical(word, 8 * pair) & 255
-                at = (2 * pair + half) * slots + start
-                count_ref[at : at + 64, :] = piece.astype(jnp.float32).astype(jnp.bfloat16)
+                two = one if two is None else two + one
+            four = plus(four, split(two, 2, 0x33333333))
+        more = [piece for word in four for piece in split(word, 4, 0x0F0F0F0F)]
+        eight = plus(eight, more)
+    pieces = []
+    for quarter in range(4):
+        for word in (eight[0], eight[2], eight[1], eight[3]):
+            piece = lax.shift_right_logical(word, 8 * quarter)
+            if quarter < 3:
+                piece = piece & 255
+            pieces.append(piece.astype(jnp.float32).astype(jnp.bfloat16))
+    return jnp.concatenate(pieces, axis=0)
+
+
+def add_rows(split_ref, table_num, codes, offset):
+    width = split_ref.shape[1] // 2
+    rows = split_ref.shape[2]
+    half = 512
+    value = None
+    for first in range(0, rows, half):
+        counts = count_rows(codes, offset, first, half)
+        for part in range(2):
+            product = jnp.dot(
+                split_ref[table_num, part * width : (part + 1) * width, first : first + half],
+                counts,
+                preferred_element_type=jnp.float32,
+            )
+            value = product if value is None else value + product
+    return value
 
 
 def visit(split, state, offset, fresh, keep):
-    tables, twice, rows = split.shape
+    tables, twice, _ = split.shape
     width = twice // 2
     samples = state.shape[1]
     head = tables * width
@@ -81,15 +108,11 @@
     entries = state.shape[0] - base
     bag = entries // tables
 
-    def kernel(split_ref, state_ref, out_ref, count_ref):
+    def kernel(split_ref, state_ref, out_ref):
         for table_num in range(tables):
             first = base + table_num * bag
             codes = state_ref[first : first + bag, :].astype(jnp.int32)
-            add_counts(codes, offset, count_ref.at[table_num])
-            both = jnp.dot(
-                split_ref[table_num], count_ref[table_num], preferred_element_type=jnp.float32
-            )
-            value = both[:width] + both[width:]
+            value = add_rows(split_ref, table_num, codes, offset)
             at = table_num * width
             if not fresh:
                 value = value + state_ref[at : at + width, :]
@@ -102,35 +125,29 @@
         out_shape=jax.ShapeDtypeStruct((head + (entries if keep else 0), samples), jnp.float32),
         in_specs=vmem(2),
         out_specs=vmem(1)[0],
-        scratch_shapes=[pltpu.VMEM((tables, rows, samples), jnp.bfloat16)],
         cost_estimate=pl.CostEstimate(flops=140_000_000, bytes_accessed=1_300_000, transcendentals=0),
         compiler_params=pltpu.CompilerParams(vmem_limit_bytes=VMEM_LIMIT),
     )(split, state)
 
 
-def join(one, two, tables):
-    height, samples = one.shape
+def deliver(pooled, tables):
+    height, samples = pooled.shape
     width = height // tables
 
-    def kernel(one_ref, two_ref, sum_ref, out_ref):
+    def kernel(pooled_ref, out_ref):
         for table_num in range(tables):
             at = table_num * width
-            value = one_ref[at : at + width, :] + two_ref[at : at + width, :]
-            sum_ref[at : at + width, :] = value
-            out_ref[:, table_num, :] = value.T
-
-    return pl.pallas_call(
-        kernel,
-        out_shape=(
-            jax.ShapeDtypeStruct((height, samples), jnp.float32),
-            jax.ShapeDtypeStruct((samples, tables, width), jnp.float32),
-        ),
-        in_specs=vmem(2),
-        out_specs=tuple(vmem(2)),
-        cost_estimate=pl.CostEstimate(flops=4_000_000, bytes_accessed=500_000, transcendentals=0),
-        compiler_params=pltpu.CompilerParams(vmem_limit_bytes=VMEM_LIMIT),
-        name="join",
-    )(one, two)
+            out_ref[:, table_num, :] = pooled_ref[at : at + width, :].T
+
+    return pl.pallas_call(
+        kernel,
+        out_shape=jax.ShapeDtypeStruct((samples, tables, width), jnp.float32),
+        in_specs=vmem(1),
+        out_specs=vmem(1)[0],
+        cost_estimate=pl.CostEstimate(flops=1_000_000, bytes_accessed=300_000, transcendentals=0),
+        compiler_params=pltpu.CompilerParams(vmem_limit_bytes=VMEM_LIMIT),
+        name="deliver",
+    )(pooled)
 
 
 def interact(pooled, gathered, width):
@@ -174,11 +191,12 @@
     ahead = shift(visit(split, ahead, 5, False, True), "blk", 1)
     back = shift(visit(split, back, 3, False, False), "blk", -1)
     ahead = visit(split, ahead, 4, False, False)
-    pooled, result = join(ahead, back, count)
-    result = shift(result, "blk", 4)
+    pooled = ahead + back
+    result = shift(pooled, "blk", 4)
     gathered = lax.all_gather(pooled, "grp", axis=0, tiled=True)
     inter = interact(pooled, gathered, width)
     inter = shift(inter, "blk", 4)
+    result = deliver(result, count)
     return result, inter.reshape(count, -1, samples).transpose(2, 0, 1)
 
 

time: 95.6 us -> 94.8 us (level)
    pallas_call x8, Pallas kernels: 8.26 us -> 7.17 us  [visit(): pl.pallas_call(kernel, out_shape=jax.ShapeDtypeStruct((head + (entries if...]
    unnamed x6 -> x5, local copies, waits for them, and re-layouts: 2.89 us -> 2.23 us
  transfers between devices with their start and end apart: 10 -> 10, of which waited for: 3 -> 3; matrix products, arithmetic and copies ran while one was open for 0% -> 0% of each run, Pallas kernels for 8% -> 7%
where the time goes in v3:
time: 94.8 us; the launch traced here: 94.3 us
  starting transfers between devices  54.2 us (57%)
  waiting for transfers between devices  15.3 us (16%)
  blocking collectives  13.4 us (14%)
  Pallas kernels  8.41 us (9%)
  local copies, waits for them, and re-layouts  2.23 us (2%)
    ppermute x10, starting transfers between devices, shift(): return lax.ppermute(value, axis, pairs)  54.2 us
    ppermute x10, waiting for transfers between devices, shift(): return lax.ppermute(value, axis, pairs)  15.3 us
    all_gather x1, blocking collectives, shards(): gathered = lax.all_gather(pooled, 'grp', axis=0, tiled=True)  13.4 us
    pallas_call x8, Pallas kernels, visit(): pl.pallas_call(kernel, out_shape=jax.ShapeDtypeStruct((head + (entries if...  7.17 us
    unnamed x5, local copies, waits for them, and re-layouts  2.23 us
  transfers between devices with their start and end apart: 10, of which 3 were waited for; matrix products, arithmetic and copies ran while one was open for 0% of the time, Pallas kernels for 7%

profile of v3, /device:TPU:1, one launch (start us, length us, event | category | flops | bytes accessed | tf_op | source)
XLA Modules:
  0.0 94.3 jit_solution(2365484829182288821)
XLA Ops:
  0.6 1.2 %copy-done = f32[2,1024,128]{2,1,0:T(8,128)S(1)} copy-done((f32[2,1024,128]{2,1,0:T(8,128)S(1)}, f32[2,1024,128]{2,1,0:T(8,128)}, u32[]{:S(2)}) %copy-start) | copy-done | bytes 1048600
  1.9 0.3 prepare.1.split_ref
  2.2 0.4 copy-done.1
  2.6 0.9 shard_map.45
  3.5 15.3 %collective-permute-start.4 = (f32[320,128]{1,0:T(8,128)S(1)}, f32[320,128]{1,0:T(8,128)S(1)}, u32[]{:S(2)}, u32[]{:S(2)}) collective-permute-start(f32[320,128]{1,0:T(8,128)S(1)} %shard_map.45), channel_id=1, source_target_pairs={{0,508},{4,0},{8,4},{12,8},{16,12},{20,16},{24,20},{28,24},{32,28}... | collective-permute-start | bytes 491528 | tf_op jit(solution)/shard_map/ppermute | solution.py:16
  18.8 6.5 %collective-permute-start = (s32[64,128]{1,0:T(8,128)S(1)}, s32[64,128]{1,0:T(8,128)S(1)}, u32[]{:S(2)}, u32[]{:S(2)}) collective-permute-start(s32[64,128]{1,0:T(8,128)S(1)} %bitcast.7), channel_id=1, source_target_pairs={{0,484},{4,488},{8,492},{12,496},{16,500},{20,504},{24,508},{28,0}... | collective-permute-start | bytes 98312 | tf_op jit(solution)/shard_map/ppermute | solution.py:16
  25.4 4.9 %collective-permute-done.state_ref = s32[64,128]{1,0:T(8,128)S(1)} collective-permute-done((s32[64,128]{1,0:T(8,128)S(1)}, s32[64,128]{1,0:T(8,128)S(1)}, u32[]{:S(2)}, u32[]{:S(2)}) %collective-permute-start) | collective-permute-done | bytes 32800 | tf_op jit(solution)/shard_map/ppermute | solution.py:16
  30.2 0.9 shard_map.41
  31.1 1.9 %collective-permute-start.1 = (f32[320,128]{1,0:T(8,128)S(1)}, f32[320,128]{1,0:T(8,128)S(1)}, u32[]{:S(2)}, u32[]{:S(2)}) collective-permute-start(f32[320,128]{1,0:T(8,128)S(1)} %shard_map.41), channel_id=1, source_target_pairs={{0,4},{4,8},{8,12},{12,16},{16,20},{20,24},{24,28},{28,32},{32,36}... | collective-permute-start | bytes 491528 | tf_op jit(solution)/shard_map/ppermute | solution.py:16
  33.1 0.0 collective-permute-done.4.state_ref
  33.1 0.9 shard_map.46
  34.0 7.6 %collective-permute-start.5 = (f32[320,128]{1,0:T(8,128)S(1)}, f32[320,128]{1,0:T(8,128)S(1)}, u32[]{:S(2)}, u32[]{:S(2)}) collective-permute-start(f32[320,128]{1,0:T(8,128)S(1)} %shard_map.46), channel_id=1, source_target_pairs={{0,508},{4,0},{8,4},{12,8},{16,12},{20,16},{24,20},{28,24},{32,28}... | collective-permute-start | bytes 491528 | tf_op jit(solution)/shard_map/ppermute | solution.py:16
  41.6 0.0 collective-permute-done.1.state_ref
  41.6 0.9 shard_map.42
  42.5 1.9 %collective-permute-start.2 = (f32[320,128]{1,0:T(8,128)S(1)}, f32[320,128]{1,0:T(8,128)S(1)}, u32[]{:S(2)}, u32[]{:S(2)}) collective-permute-start(f32[320,128]{1,0:T(8,128)S(1)} %shard_map.42), channel_id=1, source_target_pairs={{0,4},{4,8},{8,12},{12,16},{16,20},{20,24},{24,28},{28,32},{32,36}... | collective-permute-start | bytes 491528 | tf_op jit(solution)/shard_map/ppermute | solution.py:16
  44.4 0.0 collective-permute-done.5.state_ref
  44.4 0.9 shard_map.47
  45.3 7.6 %collective-permute-start.6 = (f32[320,128]{1,0:T(8,128)S(1)}, f32[320,128]{1,0:T(8,128)S(1)}, u32[]{:S(2)}, u32[]{:S(2)}) collective-permute-start(f32[320,128]{1,0:T(8,128)S(1)} %shard_map.47), channel_id=1, source_target_pairs={{0,508},{4,0},{8,4},{12,8},{16,12},{20,16},{24,20},{28,24},{32,28}... | collective-permute-start | bytes 491528 | tf_op jit(solution)/shard_map/ppermute | solution.py:16
  52.9 0.9 shard_map.43
  53.8 1.9 %collective-permute-start.3 = (f32[320,128]{1,0:T(8,128)S(1)}, f32[320,128]{1,0:T(8,128)S(1)}, u32[]{:S(2)}, u32[]{:S(2)}) collective-permute-start(f32[320,128]{1,0:T(8,128)S(1)} %shard_map.43), channel_id=1, source_target_pairs={{0,4},{4,8},{8,12},{12,16},{16,20},{20,24},{24,28},{28,32},{32,36}... | collective-permute-start | bytes 491528 | tf_op jit(solution)/shard_map/ppermute | solution.py:16
  55.7 0.9 shard_map.48
  56.6 7.6 %collective-permute-start.7 = (f32[256,128]{1,0:T(8,128)S(1)}, f32[256,128]{1,0:T(8,128)S(1)}, u32[]{:S(2)}, u32[]{:S(2)}) collective-permute-start(f32[256,128]{1,0:T(8,128)S(1)} %shard_map.48), channel_id=1, source_target_pairs={{0,508},{4,0},{8,4},{12,8},{16,12},{20,16},{24,20},{28,24},{32,28}... | collective-permute-start | bytes 393224 | tf_op jit(solution)/shard_map/ppermute | solution.py:16
  64.2 0.9 shard_map.44
  65.1 1.0 %collective-permute-done.7 = f32[256,128]{1,0:T(8,128)S(1)} collective-permute-done((f32[256,128]{1,0:T(8,128)S(1)}, f32[256,128]{1,0:T(8,128)S(1)}, u32[]{:S(2)}, u32[]{:S(2)}) %collective-permute-start.7) | collective-permute-done | bytes 131104 | tf_op jit(solution)/shard_map/ppermute | solution.py:16
  66.2 1.9 %collective-permute-start.8 = (f32[256,128]{1,0:T(8,128)S(1)}, f32[256,128]{1,0:T(8,128)S(1)}, u32[]{:S(2)}, u32[]{:S(2)}) collective-permute-start(f32[256,128]{1,0:T(8,128)S(1)} %add.3.pooled_ref), channel_id=1, source_target_pairs={{0,16},{4,20},{8,24},{12,28},{16,32},{20,36},{24,40},{28,44},{32,4... | collective-permute-start | bytes 393224 | tf_op jit(solution)/shard_map/ppermute | solution.py:16
  68.1 13.4 %all_gather.3.gathered_ref = f32[1024,128]{1,0:T(8,128)S(1)} all-gather(f32[256,128]{1,0:T(8,128)S(1)} %add.3.pooled_ref), channel_id=1, replica_groups=mesh['blk'=128,'grp'=4] {'grp'}, dimensions={0}, use_global_device_ids=true | all-gather | bytes 655360 | tf_op jit(solution)/shard_map/all_gather | solution.py:196
  81.5 0.1 interact.1
  81.6 1.9 %collective-permute-start.9 = (f32[16,128]{1,0:T(8,128)S(1)}, f32[16,128]{1,0:T(8,128)S(1)}, u32[]{:S(2)}, u32[]{:S(2)}) collective-permute-start(f32[16,128]{1,0:T(8,128)S(1)} %interact.1), channel_id=1, source_target_pairs={{0,16},{4,20},{8,24},{12,28},{16,32},{20,36},{24,40},{28,44},{32,4... | collective-permute-start | bytes 24584 | tf_op jit(solution)/shard_map/ppermute | solution.py:16
  83.5 9.4 %collective-permute-done.9 = f32[16,128]{1,0:T(8,128)S(1)} collective-permute-done((f32[16,128]{1,0:T(8,128)S(1)}, f32[16,128]{1,0:T(8,128)S(1)}, u32[]{:S(2)}, u32[]{:S(2)}) %collective-permute-start.9) | collective-permute-done | bytes 8224 | tf_op jit(solution)/shard_map/ppermute | solution.py:16
  92.9 0.0 collective-permute-done.8.pooled_ref
  92.9 0.8 deliver.1
  93.7 0.6 copy.5
  (6 shorter events, 0.0 us)
Async XLA Ops:
  0.6 1.2 %copy-start = (f32[2,1024,128]{2,1,0:T(8,128)S(1)}, f32[2,1024,128]{2,1,0:T(8,128)}, u32[]{:S(2)}) copy-start(f32[2,1024,128]{2,1,0:T(8,128)} %table_ref.1) | copy-start | bytes 3145732
  1.9 0.8 copy-start.1
  3.5 29.6 %collective-permute-start.4 = (f32[320,128]{1,0:T(8,128)S(1)}, f32[320,128]{1,0:T(8,128)S(1)}, u32[]{:S(2)}, u32[]{:S(2)}) collective-permute-start(f32[320,128]{1,0:T(8,128)S(1)} %shard_map.45), channel_id=1, source_target_pairs={{0,508},{4,0},{8,4},{12,8},{16,12},{20,16},{24,20},{28,24},{32,28}... | collective-permute-start | bytes 491528 | tf_op jit(solution)/shard_map/ppermute | solution.py:16
  18.8 11.4 %collective-permute-start = (s32[64,128]{1,0:T(8,128)S(1)}, s32[64,128]{1,0:T(8,128)S(1)}, u32[]{:S(2)}, u32[]{:S(2)}) collective-permute-start(s32[64,128]{1,0:T(8,128)S(1)} %bitcast.7), channel_id=1, source_target_pairs={{0,484},{4,488},{8,492},{12,496},{16,500},{20,504},{24,508},{28,0}... | collective-permute-start | bytes 98312 | tf_op jit(solution)/shard_map/ppermute | solution.py:16
  31.1 10.4 %collective-permute-start.1 = (f32[320,128]{1,0:T(8,128)S(1)}, f32[320,128]{1,0:T(8,128)S(1)}, u32[]{:S(2)}, u32[]{:S(2)}) collective-permute-start(f32[320,128]{1,0:T(8,128)S(1)} %shard_map.41), channel_id=1, source_target_pairs={{0,4},{4,8},{8,12},{12,16},{16,20},{20,24},{24,28},{28,32},{32,36}... | collective-permute-start | bytes 491528 | tf_op jit(solution)/shard_map/ppermute | solution.py:16
  34.0 10.4 %collective-permute-start.5 = (f32[320,128]{1,0:T(8,128)S(1)}, f32[320,128]{1,0:T(8,128)S(1)}, u32[]{:S(2)}, u32[]{:S(2)}) collective-permute-start(f32[320,128]{1,0:T(8,128)S(1)} %shard_map.46), channel_id=1, source_target_pairs={{0,508},{4,0},{8,4},{12,8},{16,12},{20,16},{24,20},{28,24},{32,28}... | collective-permute-start | bytes 491528 | tf_op jit(solution)/shard_map/ppermute | solution.py:16
  42.5 10.4 %collective-permute-start.2 = (f32[320,128]{1,0:T(8,128)S(1)}, f32[320,128]{1,0:T(8,128)S(1)}, u32[]{:S(2)}, u32[]{:S(2)}) collective-permute-start(f32[320,128]{1,0:T(8,128)S(1)} %shard_map.42), channel_id=1, source_target_pairs={{0,4},{4,8},{8,12},{12,16},{16,20},{20,24},{24,28},{28,32},{32,36}... | collective-permute-start | bytes 491528 | tf_op jit(solution)/shard_map/ppermute | solution.py:16
  45.3 10.4 %collective-permute-start.6 = (f32[320,128]{1,0:T(8,128)S(1)}, f32[320,128]{1,0:T(8,128)S(1)}, u32[]{:S(2)}, u32[]{:S(2)}) collective-permute-start(f32[320,128]{1,0:T(8,128)S(1)} %shard_map.47), channel_id=1, source_target_pairs={{0,508},{4,0},{8,4},{12,8},{16,12},{20,16},{24,20},{28,24},{32,28}... | collective-permute-start | bytes 491528 | tf_op jit(solution)/shard_map/ppermute | solution.py:16
  53.8 10.4 %collective-permute-start.3 = (f32[320,128]{1,0:T(8,128)S(1)}, f32[320,128]{1,0:T(8,128)S(1)}, u32[]{:S(2)}, u32[]{:S(2)}) collective-permute-start(f32[320,128]{1,0:T(8,128)S(1)} %shard_map.43), channel_id=1, source_target_pairs={{0,4},{4,8},{8,12},{12,16},{16,20},{20,24},{24,28},{28,32},{32,36}... | collective-permute-start | bytes 491528 | tf_op jit(solution)/shard_map/ppermute | solution.py:16
  56.6 9.5 %collective-permute-start.7 = (f32[256,128]{1,0:T(8,128)S(1)}, f32[256,128]{1,0:T(8,128)S(1)}, u32[]{:S(2)}, u32[]{:S(2)}) collective-permute-start(f32[256,128]{1,0:T(8,128)S(1)} %shard_map.48), channel_id=1, source_target_pairs={{0,508},{4,0},{8,4},{12,8},{16,12},{20,16},{24,20},{28,24},{32,28}... | collective-permute-start | bytes 393224 | tf_op jit(solution)/shard_map/ppermute | solution.py:16
  66.2 26.7 %collective-permute-start.8 = (f32[256,128]{1,0:T(8,128)S(1)}, f32[256,128]{1,0:T(8,128)S(1)}, u32[]{:S(2)}, u32[]{:S(2)}) collective-permute-start(f32[256,128]{1,0:T(8,128)S(1)} %add.3.pooled_ref), channel_id=1, source_target_pairs={{0,16},{4,20},{8,24},{12,28},{16,32},{20,36},{24,40},{28,44},{32,4... | collective-permute-start | bytes 393224 | tf_op jit(solution)/shard_map/ppermute | solution.py:16
  81.6 11.3 %collective-permute-start.9 = (f32[16,128]{1,0:T(8,128)S(1)}, f32[16,128]{1,0:T(8,128)S(1)}, u32[]{:S(2)}, u32[]{:S(2)}) collective-permute-start(f32[16,128]{1,0:T(8,128)S(1)} %interact.1), channel_id=1, source_target_pairs={{0,16},{4,20},{8,24},{12,28},{16,32},{20,36},{24,40},{28,44},{32,4... | collective-permute-start | bytes 24584 | tf_op jit(solution)/shard_map/ppermute | solution.py:16

commit v4 on v3

--- a/solution.py
+++ b/solution.py
@@ -43,15 +43,19 @@
     )(tables)
 
 
-def count_rows(codes, offset, first_row, height):
-    samples = codes.shape[1]
-    entries = codes.shape[0]
-    slots = height // 16
-    row = lax.shift_right_logical(codes, 3) - first_row
-    hit = ((codes & (SECTIONS - 1)) == offset) & (row >= 0) & (row < height)
-    slot = jnp.where(hit, row & (slots - 1), -1)
-    unit = jnp.left_shift(1, lax.shift_right_logical(row, slots.bit_length() - 1) * 2 & 31)
-    place = lax.broadcasted_iota(jnp.int32, (slots, samples), 0)
+def place_ids(codes, offset, slot_ref, unit_ref):
+    row = lax.shift_right_logical(codes, 3)
+    slot = (row & 31) | (lax.shift_right_logical(row, 9) << 5)
+    slot_ref[...] = jnp.where((codes & (SECTIONS - 1)) == offset, slot, -1)
+    unit_ref[...] = jnp.left_shift(1, (lax.shift_right_logical(row, 5) & 15) * 2)
+
+
+def count_rows(slot_ref, unit_ref, first, entries, chunk):
+    samples = slot_ref.shape[1]
+    place = lax.broadcasted_iota(jnp.int32, (32, samples), 0) + 32 * chunk
+
+    def row_of(ref, entry):
+        return jnp.broadcast_to(ref[first + entry : first + entry + 1, :], (32, samples))
 
     def plus(total, more):
         return more if total is None else [x + y for x, y in zip(total, more)]
@@ -60,13 +64,13 @@
         return [word & mask, lax.shift_right_logical(word, bits) & mask]
 
     eight = None
-    for first in range(0, entries, 15):
+    for block in range(0, entries, 15):
         four = None
-        for start in range(first, min(first + 15, entries), 3):
+        for start in range(block, min(block + 15, entries), 3):
             two = None
             for entry in range(start, min(start + 3, entries)):
                 one = jnp.where(
-                    place == slot[entry : entry + 1, :], unit[entry : entry + 1, :], 0
+                    place == row_of(slot_ref, entry), row_of(unit_ref, entry), 0
                 )
                 two = one if two is None else two + one
             four = plus(four, split(two, 2, 0x33333333))
@@ -82,21 +86,19 @@
     return jnp.concatenate(pieces, axis=0)
 
 
-def add_rows(split_ref, table_num, codes, offset):
+def add_rows(split_ref, table_num, slot_ref, unit_ref, bag):
     width = split_ref.shape[1] // 2
     rows = split_ref.shape[2]
-    half = 512
     value = None
-    for first in range(0, rows, half):
-        counts = count_rows(codes, offset, first, half)
-        for part in range(2):
-            product = jnp.dot(
-                split_ref[table_num, part * width : (part + 1) * width, first : first + half],
-                counts,
-                preferred_element_type=jnp.float32,
-            )
-            value = product if value is None else value + product
-    return value
+    for chunk in range(rows // 512):
+        counts = count_rows(slot_ref, unit_ref, table_num * bag, bag, chunk)
+        both = jnp.dot(
+            split_ref[table_num, :, chunk * 512 : (chunk + 1) * 512],
+            counts,
+            preferred_element_type=jnp.float32,
+        )
+        value = both if value is None else value + both
+    return value[:width] + value[width:]
 
 
 def visit(split, state, offset, fresh, keep):
@@ -108,11 +110,10 @@
     entries = state.shape[0] - base
     bag = entries // tables
 
-    def kernel(split_ref, state_ref, out_ref):
+    def kernel(split_ref, state_ref, out_ref, slot_ref, unit_ref):
+        place_ids(state_ref[base:, :].astype(jnp.int32), offset, slot_ref, unit_ref)
         for table_num in range(tables):
-            first = base + table_num * bag
-            codes = state_ref[first : first + bag, :].astype(jnp.int32)
-            value = add_rows(split_ref, table_num, codes, offset)
+            value = add_rows(split_ref, table_num, slot_ref, unit_ref, bag)
             at = table_num * width
             if not fresh:
                 value = value + state_ref[at : at + width, :]
@@ -125,6 +126,7 @@
         out_shape=jax.ShapeDtypeStruct((head + (entries if keep else 0), samples), jnp.float32),
         in_specs=vmem(2),
         out_specs=vmem(1)[0],
+        scratch_shapes=[pltpu.VMEM((entries, samples), jnp.int32)] * 2,
         cost_estimate=pl.CostEstimate(flops=140_000_000, bytes_accessed=1_300_000, transcendentals=0),
         compiler_params=pltpu.CompilerParams(vmem_limit_bytes=VMEM_LIMIT),
     )(split, state)

time: 94.8 us -> 94.7 us (level)
  no operation moved by 1% of the time
where the time goes in v4:
time: 94.7 us; the launch traced here: 94.2 us
  starting transfers between devices  54.2 us (57%)
  waiting for transfers between devices  15.3 us (16%)
  blocking collectives  13.4 us (14%)
  Pallas kernels  8.18 us (9%)
  local copies, waits for them, and re-layouts  2.23 us (2%)
    ppermute x10, starting transfers between devices, shift(): return lax.ppermute(value, axis, pairs)  54.2 us
    ppermute x10, waiting for transfers between devices, shift(): return lax.ppermute(value, axis, pairs)  15.3 us
    all_gather x1, blocking collectives, shards(): gathered = lax.all_gather(pooled, 'grp', axis=0, tiled=True)  13.4 us
    pallas_call x8, Pallas kernels, visit(): pl.pallas_call(kernel, out_shape=jax.ShapeDtypeStruct((head + (entries if...  6.94 us
    unnamed x5, local copies, waits for them, and re-layouts  2.23 us
  transfers between devices with their start and end apart: 10, of which 3 were waited for; matrix products, arithmetic and copies ran while one was open for 0% of the time, Pallas kernels for 7%

profile of v4, /device:TPU:1, one launch (start us, length us, event | category | flops | bytes accessed | tf_op | source)
XLA Modules:
  0.0 94.2 jit_solution(10237104682817973532)
XLA Ops:
  0.6 1.2 %copy-done = f32[2,1024,128]{2,1,0:T(8,128)S(1)} copy-done((f32[2,1024,128]{2,1,0:T(8,128)S(1)}, f32[2,1024,128]{2,1,0:T(8,128)}, u32[]{:S(2)}) %copy-start) | copy-done | bytes 1048600
  1.9 0.3 prepare.1.split_ref
  2.2 0.4 copy-done.1
  2.6 0.9 shard_map.45
  3.5 15.3 %collective-permute-start.4 = (f32[320,128]{1,0:T(8,128)S(1)}, f32[320,128]{1,0:T(8,128)S(1)}, u32[]{:S(2)}, u32[]{:S(2)}) collective-permute-start(f32[320,128]{1,0:T(8,128)S(1)} %shard_map.45), channel_id=1, source_target_pairs={{0,508},{4,0},{8,4},{12,8},{16,12},{20,16},{24,20},{28,24},{32,28}... | collective-permute-start | bytes 491528 | tf_op jit(solution)/shard_map/ppermute | solution.py:16
  18.8 6.5 %collective-permute-start = (s32[64,128]{1,0:T(8,128)S(1)}, s32[64,128]{1,0:T(8,128)S(1)}, u32[]{:S(2)}, u32[]{:S(2)}) collective-permute-start(s32[64,128]{1,0:T(8,128)S(1)} %bitcast.7), channel_id=1, source_target_pairs={{0,484},{4,488},{8,492},{12,496},{16,500},{20,504},{24,508},{28,0}... | collective-permute-start | bytes 98312 | tf_op jit(solution)/shard_map/ppermute | solution.py:16
  25.3 4.9 %collective-permute-done.state_ref = s32[64,128]{1,0:T(8,128)S(1)} collective-permute-done((s32[64,128]{1,0:T(8,128)S(1)}, s32[64,128]{1,0:T(8,128)S(1)}, u32[]{:S(2)}, u32[]{:S(2)}) %collective-permute-start) | collective-permute-done | bytes 32800 | tf_op jit(solution)/shard_map/ppermute | solution.py:16
  30.2 0.9 shard_map.41
  31.1 1.9 %collective-permute-start.1 = (f32[320,128]{1,0:T(8,128)S(1)}, f32[320,128]{1,0:T(8,128)S(1)}, u32[]{:S(2)}, u32[]{:S(2)}) collective-permute-start(f32[320,128]{1,0:T(8,128)S(1)} %shard_map.41), channel_id=1, source_target_pairs={{0,4},{4,8},{8,12},{12,16},{16,20},{20,24},{24,28},{28,32},{32,36}... | collective-permute-start | bytes 491528 | tf_op jit(solution)/shard_map/ppermute | solution.py:16
  33.1 0.9 shard_map.46
  33.9 7.6 %collective-permute-start.5 = (f32[320,128]{1,0:T(8,128)S(1)}, f32[320,128]{1,0:T(8,128)S(1)}, u32[]{:S(2)}, u32[]{:S(2)}) collective-permute-start(f32[320,128]{1,0:T(8,128)S(1)} %shard_map.46), channel_id=1, source_target_pairs={{0,508},{4,0},{8,4},{12,8},{16,12},{20,16},{24,20},{28,24},{32,28}... | collective-permute-start | bytes 491528 | tf_op jit(solution)/shard_map/ppermute | solution.py:16
  41.5 0.0 collective-permute-done.1.state_ref
  41.5 0.9 shard_map.42
  42.4 1.9 %collective-permute-start.2 = (f32[320,128]{1,0:T(8,128)S(1)}, f32[320,128]{1,0:T(8,128)S(1)}, u32[]{:S(2)}, u32[]{:S(2)}) collective-permute-start(f32[320,128]{1,0:T(8,128)S(1)} %shard_map.42), channel_id=1, source_target_pairs={{0,4},{4,8},{8,12},{12,16},{16,20},{20,24},{24,28},{28,32},{32,36}... | collective-permute-start | bytes 491528 | tf_op jit(solution)/shard_map/ppermute | solution.py:16
  44.3 0.0 collective-permute-done.5.state_ref
  44.3 0.9 shard_map.47
  45.2 7.6 %collective-permute-start.6 = (f32[320,128]{1,0:T(8,128)S(1)}, f32[320,128]{1,0:T(8,128)S(1)}, u32[]{:S(2)}, u32[]{:S(2)}) collective-permute-start(f32[320,128]{1,0:T(8,128)S(1)} %shard_map.47), channel_id=1, source_target_pairs={{0,508},{4,0},{8,4},{12,8},{16,12},{20,16},{24,20},{28,24},{32,28}... | collective-permute-start | bytes 491528 | tf_op jit(solution)/shard_map/ppermute | solution.py:16
  52.8 0.9 shard_map.43
  53.7 1.9 %collective-permute-start.3 = (f32[320,128]{1,0:T(8,128)S(1)}, f32[320,128]{1,0:T(8,128)S(1)}, u32[]{:S(2)}, u32[]{:S(2)}) collective-permute-start(f32[320,128]{1,0:T(8,128)S(1)} %shard_map.43), channel_id=1, source_target_pairs={{0,4},{4,8},{8,12},{12,16},{16,20},{20,24},{24,28},{28,32},{32,36}... | collective-permute-start | bytes 491528 | tf_op jit(solution)/shard_map/ppermute | solution.py:16
  55.6 0.9 shard_map.48
  56.5 7.6 %collective-permute-start.7 = (f32[256,128]{1,0:T(8,128)S(1)}, f32[256,128]{1,0:T(8,128)S(1)}, u32[]{:S(2)}, u32[]{:S(2)}) collective-permute-start(f32[256,128]{1,0:T(8,128)S(1)} %shard_map.48), channel_id=1, source_target_pairs={{0,508},{4,0},{8,4},{12,8},{16,12},{20,16},{24,20},{28,24},{32,28}... | collective-permute-start | bytes 393224 | tf_op jit(solution)/shard_map/ppermute | solution.py:16
  64.1 0.0 collective-permute-done.3.state_ref
  64.1 0.9 shard_map.44
  65.0 1.0 %collective-permute-done.7 = f32[256,128]{1,0:T(8,128)S(1)} collective-permute-done((f32[256,128]{1,0:T(8,128)S(1)}, f32[256,128]{1,0:T(8,128)S(1)}, u32[]{:S(2)}, u32[]{:S(2)}) %collective-permute-start.7) | collective-permute-done | bytes 131104 | tf_op jit(solution)/shard_map/ppermute | solution.py:16
  66.0 1.9 %collective-permute-start.8 = (f32[256,128]{1,0:T(8,128)S(1)}, f32[256,128]{1,0:T(8,128)S(1)}, u32[]{:S(2)}, u32[]{:S(2)}) collective-permute-start(f32[256,128]{1,0:T(8,128)S(1)} %add.3.pooled_ref), channel_id=1, source_target_pairs={{0,16},{4,20},{8,24},{12,28},{16,32},{20,36},{24,40},{28,44},{32,4... | collective-permute-start | bytes 393224 | tf_op jit(solution)/shard_map/ppermute | solution.py:16
  67.9 13.4 %all_gather.3.gathered_ref = f32[1024,128]{1,0:T(8,128)S(1)} all-gather(f32[256,128]{1,0:T(8,128)S(1)} %add.3.pooled_ref), channel_id=1, replica_groups=mesh['blk'=128,'grp'=4] {'grp'}, dimensions={0}, use_global_device_ids=true | all-gather | bytes 655360 | tf_op jit(solution)/shard_map/all_gather | solution.py:198
  81.3 0.1 interact.1
  81.4 1.9 %collective-permute-start.9 = (f32[16,128]{1,0:T(8,128)S(1)}, f32[16,128]{1,0:T(8,128)S(1)}, u32[]{:S(2)}, u32[]{:S(2)}) collective-permute-start(f32[16,128]{1,0:T(8,128)S(1)} %interact.1), channel_id=1, source_target_pairs={{0,16},{4,20},{8,24},{12,28},{16,32},{20,36},{24,40},{28,44},{32,4... | collective-permute-start | bytes 24584 | tf_op jit(solution)/shard_map/ppermute | solution.py:16
  83.4 9.4 %collective-permute-done.9 = f32[16,128]{1,0:T(8,128)S(1)} collective-permute-done((f32[16,128]{1,0:T(8,128)S(1)}, f32[16,128]{1,0:T(8,128)S(1)}, u32[]{:S(2)}, u32[]{:S(2)}) %collective-permute-start.9) | collective-permute-done | bytes 8224 | tf_op jit(solution)/shard_map/ppermute | solution.py:16
  92.8 0.0 collective-permute-done.8.pooled_ref
  92.8 0.8 deliver.1
  93.6 0.6 copy.5
  (6 shorter events, 0.0 us)
Async XLA Ops:
  0.6 1.2 %copy-start = (f32[2,1024,128]{2,1,0:T(8,128)S(1)}, f32[2,1024,128]{2,1,0:T(8,128)}, u32[]{:S(2)}) copy-start(f32[2,1024,128]{2,1,0:T(8,128)} %table_ref.1) | copy-start | bytes 3145732
  1.9 0.8 copy-start.1
  3.5 29.5 %collective-permute-start.4 = (f32[320,128]{1,0:T(8,128)S(1)}, f32[320,128]{1,0:T(8,128)S(1)}, u32[]{:S(2)}, u32[]{:S(2)}) collective-permute-start(f32[320,128]{1,0:T(8,128)S(1)} %shard_map.45), channel_id=1, source_target_pairs={{0,508},{4,0},{8,4},{12,8},{16,12},{20,16},{24,20},{28,24},{32,28}... | collective-permute-start | bytes 491528 | tf_op jit(solution)/shard_map/ppermute | solution.py:16
  18.8 11.4 %collective-permute-start = (s32[64,128]{1,0:T(8,128)S(1)}, s32[64,128]{1,0:T(8,128)S(1)}, u32[]{:S(2)}, u32[]{:S(2)}) collective-permute-start(s32[64,128]{1,0:T(8,128)S(1)} %bitcast.7), channel_id=1, source_target_pairs={{0,484},{4,488},{8,492},{12,496},{16,500},{20,504},{24,508},{28,0}... | collective-permute-start | bytes 98312 | tf_op jit(solution)/shard_map/ppermute | solution.py:16
  31.1 10.4 %collective-permute-start.1 = (f32[320,128]{1,0:T(8,128)S(1)}, f32[320,128]{1,0:T(8,128)S(1)}, u32[]{:S(2)}, u32[]{:S(2)}) collective-permute-start(f32[320,128]{1,0:T(8,128)S(1)} %shard_map.41), channel_id=1, source_target_pairs={{0,4},{4,8},{8,12},{12,16},{16,20},{20,24},{24,28},{28,32},{32,36}... | collective-permute-start | bytes 491528 | tf_op jit(solution)/shard_map/ppermute | solution.py:16
  33.9 10.4 %collective-permute-start.5 = (f32[320,128]{1,0:T(8,128)S(1)}, f32[320,128]{1,0:T(8,128)S(1)}, u32[]{:S(2)}, u32[]{:S(2)}) collective-permute-start(f32[320,128]{1,0:T(8,128)S(1)} %shard_map.46), channel_id=1, source_target_pairs={{0,508},{4,0},{8,4},{12,8},{16,12},{20,16},{24,20},{28,24},{32,28}... | collective-permute-start | bytes 491528 | tf_op jit(solution)/shard_map/ppermute | solution.py:16
  42.4 10.4 %collective-permute-start.2 = (f32[320,128]{1,0:T(8,128)S(1)}, f32[320,128]{1,0:T(8,128)S(1)}, u32[]{:S(2)}, u32[]{:S(2)}) collective-permute-start(f32[320,128]{1,0:T(8,128)S(1)} %shard_map.42), channel_id=1, source_target_pairs={{0,4},{4,8},{8,12},{12,16},{16,20},{20,24},{24,28},{28,32},{32,36}... | collective-permute-start | bytes 491528 | tf_op jit(solution)/shard_map/ppermute | solution.py:16
  45.2 10.4 %collective-permute-start.6 = (f32[320,128]{1,0:T(8,128)S(1)}, f32[320,128]{1,0:T(8,128)S(1)}, u32[]{:S(2)}, u32[]{:S(2)}) collective-permute-start(f32[320,128]{1,0:T(8,128)S(1)} %shard_map.47), channel_id=1, source_target_pairs={{0,508},{4,0},{8,4},{12,8},{16,12},{20,16},{24,20},{28,24},{32,28}... | collective-permute-start | bytes 491528 | tf_op jit(solution)/shard_map/ppermute | solution.py:16
  53.7 10.4 %collective-permute-start.3 = (f32[320,128]{1,0:T(8,128)S(1)}, f32[320,128]{1,0:T(8,128)S(1)}, u32[]{:S(2)}, u32[]{:S(2)}) collective-permute-start(f32[320,128]{1,0:T(8,128)S(1)} %shard_map.43), channel_id=1, source_target_pairs={{0,4},{4,8},{8,12},{12,16},{16,20},{20,24},{24,28},{28,32},{32,36}... | collective-permute-start | bytes 491528 | tf_op jit(solution)/shard_map/ppermute | solution.py:16
  56.5 9.5 %collective-permute-start.7 = (f32[256,128]{1,0:T(8,128)S(1)}, f32[256,128]{1,0:T(8,128)S(1)}, u32[]{:S(2)}, u32[]{:S(2)}) collective-permute-start(f32[256,128]{1,0:T(8,128)S(1)} %shard_map.48), channel_id=1, source_target_pairs={{0,508},{4,0},{8,4},{12,8},{16,12},{20,16},{24,20},{28,24},{32,28}... | collective-permute-start | bytes 393224 | tf_op jit(solution)/shard_map/ppermute | solution.py:16
  66.0 26.8 %collective-permute-start.8 = (f32[256,128]{1,0:T(8,128)S(1)}, f32[256,128]{1,0:T(8,128)S(1)}, u32[]{:S(2)}, u32[]{:S(2)}) collective-permute-start(f32[256,128]{1,0:T(8,128)S(1)} %add.3.pooled_ref), channel_id=1, source_target_pairs={{0,16},{4,20},{8,24},{12,28},{16,32},{20,36},{24,40},{28,44},{32,4... | collective-permute-start | bytes 393224 | tf_op jit(solution)/shard_map/ppermute | solution.py:16
  81.4 11.3 %collective-permute-start.9 = (f32[16,128]{1,0:T(8,128)S(1)}, f32[16,128]{1,0:T(8,128)S(1)}, u32[]{:S(2)}, u32[]{:S(2)}) collective-permute-start(f32[16,128]{1,0:T(8,128)S(1)} %interact.1), channel_id=1, source_target_pairs={{0,16},{4,20},{8,24},{12,28},{16,32},{20,36},{24,40},{28,44},{32,4... | collective-permute-start | bytes 24584 | tf_op jit(solution)/shard_map/ppermute | solution.py:16

commit v5 on v4

--- a/solution.py
+++ b/solution.py
@@ -152,29 +152,42 @@
     )(pooled)
 
 
-def interact(pooled, gathered, width):
-    samples = pooled.shape[1]
-    tables = pooled.shape[0] // width
-    others = gathered.shape[0] // width
-
-    def kernel(pooled_ref, gathered_ref, inter_ref):
-        rows = []
+def interact(parts, order, width):
+    samples = parts[0].shape[1]
+    tables = parts[0].shape[0] // width
+
+    def kernel(order_ref, own_ref, all_ref, inter_ref):
+        rows = {}
         for table_num in range(tables):
-            own = pooled_ref[table_num * width : (table_num + 1) * width, :]
-            for other in range(others):
-                there = gathered_ref[other * width : (other + 1) * width, :]
-                rows.append(jnp.sum(own * there, axis=0, keepdims=True))
-        inter_ref[...] = jnp.concatenate(rows, axis=0) / width
-
-    return pl.pallas_call(
-        kernel,
-        out_shape=jax.ShapeDtypeStruct((tables * others, samples), jnp.float32),
-        in_specs=vmem(2),
+            own = own_ref[table_num * width : (table_num + 1) * width, :]
+            for core in range(2):
+                for place in range(2):
+                    for one in range(tables):
+                        at = ((core * 2 + place) * tables + one) * width
+                        there = all_ref[at : at + width, :]
+                        rows[table_num, place, core * tables + one] = jnp.sum(
+                            own * there, axis=0, keepdims=True
+                        )
+
+        def stacked(first, second):
+            pieces = []
+            for table_num in range(tables):
+                for place in (first, second):
+                    for other in range(2 * tables):
+                        pieces.append(rows[table_num, place, other])
+            return jnp.concatenate(pieces, axis=0) / width
+
+        inter_ref[...] = jnp.where(order_ref[0] == 0, stacked(0, 1), stacked(1, 0))
+
+    return pl.pallas_call(
+        kernel,
+        out_shape=jax.ShapeDtypeStruct((tables * 4 * tables, samples), jnp.float32),
+        in_specs=[pl.BlockSpec(memory_space=pltpu.SMEM)] + vmem(2),
         out_specs=vmem(1)[0],
         cost_estimate=pl.CostEstimate(flops=4_000_000, bytes_accessed=700_000, transcendentals=0),
         compiler_params=pltpu.CompilerParams(vmem_limit_bytes=VMEM_LIMIT),
         name="interact",
-    )(pooled, gathered)
+    )(order, *parts)
 
 
 def shards(tables, bag_ids):
@@ -195,8 +208,11 @@
     ahead = visit(split, ahead, 4, False, False)
     pooled = ahead + back
     result = shift(pooled, "blk", 4)
-    gathered = lax.all_gather(pooled, "grp", axis=0, tiled=True)
-    inter = interact(pooled, gathered, width)
+    cross = shift(pooled, "grp", 2)
+    both = jnp.concatenate([pooled, cross], axis=0)
+    gathered = lax.all_gather(both, "grp", axis=0, tiled=True, axis_index_groups=[[0, 1], [2, 3]])
+    order = lax.axis_index("grp")[None] // 2
+    inter = interact((pooled, gathered), order, width)
     inter = shift(inter, "blk", 4)
     result = deliver(result, count)
     return result, inter.reshape(count, -1, samples).transpose(2, 0, 1)

time: 94.7 us -> 94 us (level)
  blocking collectives: 13.4 us -> 8.23 us
  starting transfers between devices: 54.2 us -> 58.6 us
    all_gather x1, blocking collectives: 13.4 us -> 8.23 us  [shards(): lax.all_gather(both, 'grp', axis=0, tiled=True, axis_index_groups=[[0, 1]...]
    ppermute x10 -> x11, starting transfers between devices: 54.2 us -> 58.6 us  [shift(): return lax.ppermute(value, axis, pairs)]
    ppermute x10 -> x11, waiting for transfers between devices: 15.3 us -> 15.4 us  [shift(): return lax.ppermute(value, axis, pairs)]
  transfers between devices with their start and end apart: 10 -> 11, of which waited for: 3 -> 5; matrix products, arithmetic and copies ran while one was open for 0% -> 0% of each run, Pallas kernels for 7% -> 7%
where the time goes in v5:
time: 94 us; the launch traced here: 93.5 us
  starting transfers between devices  58.6 us (62%)
  waiting for transfers between devices  15.4 us (16%)
  blocking collectives  8.23 us (9%)
  Pallas kernels  8.18 us (9%)
  local copies, waits for them, and re-layouts  2.23 us (2%)
    ppermute x11, starting transfers between devices, shift(): return lax.ppermute(value, axis, pairs)  58.6 us
    ppermute x11, waiting for transfers between devices, shift(): return lax.ppermute(value, axis, pairs)  15.4 us
    all_gather x1, blocking collectives, shards(): lax.all_gather(both, 'grp', axis=0, tiled=True, axis_index_groups=[[0, 1]...  8.23 us
    pallas_call x8, Pallas kernels, visit(): pl.pallas_call(kernel, out_shape=jax.ShapeDtypeStruct((head + (entries if...  6.94 us
    unnamed x5, local copies, waits for them, and re-layouts  2.23 us
  transfers between devices with their start and end apart: 11, of which 5 were waited for; matrix products, arithmetic and copies ran while one was open for 0% of the time, Pallas kernels for 7%

profile of v5, /device:TPU:1, one launch (start us, length us, event | category | flops | bytes accessed | tf_op | source)
XLA Modules:
  0.0 93.5 jit_solution(3366491813700050844)
XLA Ops:
  0.6 1.2 %copy-done = f32[2,1024,128]{2,1,0:T(8,128)S(1)} copy-done((f32[2,1024,128]{2,1,0:T(8,128)S(1)}, f32[2,1024,128]{2,1,0:T(8,128)}, u32[]{:S(2)}) %copy-start) | copy-done | bytes 1048600
  1.9 0.3 prepare.1.split_ref
  2.2 0.4 copy-done.1
  2.6 0.9 shard_map.45
  3.5 15.3 %collective-permute-start.4 = (f32[320,128]{1,0:T(8,128)S(1)}, f32[320,128]{1,0:T(8,128)S(1)}, u32[]{:S(2)}, u32[]{:S(2)}) collective-permute-start(f32[320,128]{1,0:T(8,128)S(1)} %shard_map.45), channel_id=1, source_target_pairs={{0,508},{4,0},{8,4},{12,8},{16,12},{20,16},{24,20},{28,24},{32,28}... | collective-permute-start | bytes 491528 | tf_op jit(solution)/shard_map/ppermute | solution.py:16
  18.8 6.5 %collective-permute-start = (s32[64,128]{1,0:T(8,128)S(1)}, s32[64,128]{1,0:T(8,128)S(1)}, u32[]{:S(2)}, u32[]{:S(2)}) collective-permute-start(s32[64,128]{1,0:T(8,128)S(1)} %bitcast.8), channel_id=1, source_target_pairs={{0,484},{4,488},{8,492},{12,496},{16,500},{20,504},{24,508},{28,0}... | collective-permute-start | bytes 98312 | tf_op jit(solution)/shard_map/ppermute | solution.py:16
  25.3 4.9 %collective-permute-done.state_ref = s32[64,128]{1,0:T(8,128)S(1)} collective-permute-done((s32[64,128]{1,0:T(8,128)S(1)}, s32[64,128]{1,0:T(8,128)S(1)}, u32[]{:S(2)}, u32[]{:S(2)}) %collective-permute-start) | collective-permute-done | bytes 32800 | tf_op jit(solution)/shard_map/ppermute | solution.py:16
  30.2 0.9 shard_map.41
  31.1 1.9 %collective-permute-start.1 = (f32[320,128]{1,0:T(8,128)S(1)}, f32[320,128]{1,0:T(8,128)S(1)}, u32[]{:S(2)}, u32[]{:S(2)}) collective-permute-start(f32[320,128]{1,0:T(8,128)S(1)} %shard_map.41), channel_id=1, source_target_pairs={{0,4},{4,8},{8,12},{12,16},{16,20},{20,24},{24,28},{28,32},{32,36}... | collective-permute-start | bytes 491528 | tf_op jit(solution)/shard_map/ppermute | solution.py:16
  33.1 0.9 shard_map.46
  33.9 7.6 %collective-permute-start.5 = (f32[320,128]{1,0:T(8,128)S(1)}, f32[320,128]{1,0:T(8,128)S(1)}, u32[]{:S(2)}, u32[]{:S(2)}) collective-permute-start(f32[320,128]{1,0:T(8,128)S(1)} %shard_map.46), channel_id=1, source_target_pairs={{0,508},{4,0},{8,4},{12,8},{16,12},{20,16},{24,20},{28,24},{32,28}... | collective-permute-start | bytes 491528 | tf_op jit(solution)/shard_map/ppermute | solution.py:16
  41.5 0.0 collective-permute-done.1.state_ref
  41.5 0.9 shard_map.42
  42.4 1.9 %collective-permute-start.2 = (f32[320,128]{1,0:T(8,128)S(1)}, f32[320,128]{1,0:T(8,128)S(1)}, u32[]{:S(2)}, u32[]{:S(2)}) collective-permute-start(f32[320,128]{1,0:T(8,128)S(1)} %shard_map.42), channel_id=1, source_target_pairs={{0,4},{4,8},{8,12},{12,16},{16,20},{20,24},{24,28},{28,32},{32,36}... | collective-permute-start | bytes 491528 | tf_op jit(solution)/shard_map/ppermute | solution.py:16
  44.3 0.9 shard_map.47
  45.2 7.6 %collective-permute-start.6 = (f32[320,128]{1,0:T(8,128)S(1)}, f32[320,128]{1,0:T(8,128)S(1)}, u32[]{:S(2)}, u32[]{:S(2)}) collective-permute-start(f32[320,128]{1,0:T(8,128)S(1)} %shard_map.47), channel_id=1, source_target_pairs={{0,508},{4,0},{8,4},{12,8},{16,12},{20,16},{24,20},{28,24},{32,28}... | collective-permute-start | bytes 491528 | tf_op jit(solution)/shard_map/ppermute | solution.py:16
  52.8 0.9 shard_map.43
  53.7 1.9 %collective-permute-start.3 = (f32[320,128]{1,0:T(8,128)S(1)}, f32[320,128]{1,0:T(8,128)S(1)}, u32[]{:S(2)}, u32[]{:S(2)}) collective-permute-start(f32[320,128]{1,0:T(8,128)S(1)} %shard_map.43), channel_id=1, source_target_pairs={{0,4},{4,8},{8,12},{12,16},{16,20},{20,24},{24,28},{28,32},{32,36}... | collective-permute-start | bytes 491528 | tf_op jit(solution)/shard_map/ppermute | solution.py:16
  55.6 0.9 shard_map.48
  56.5 7.6 %collective-permute-start.7 = (f32[256,128]{1,0:T(8,128)S(1)}, f32[256,128]{1,0:T(8,128)S(1)}, u32[]{:S(2)}, u32[]{:S(2)}) collective-permute-start(f32[256,128]{1,0:T(8,128)S(1)} %shard_map.48), channel_id=1, source_target_pairs={{0,508},{4,0},{8,4},{12,8},{16,12},{20,16},{24,20},{28,24},{32,28}... | collective-permute-start | bytes 393224 | tf_op jit(solution)/shard_map/ppermute | solution.py:16
  64.1 0.9 shard_map.44
  65.0 1.0 %collective-permute-done.7 = f32[256,128]{1,0:T(8,128)S(1)} collective-permute-done((f32[256,128]{1,0:T(8,128)S(1)}, f32[256,128]{1,0:T(8,128)S(1)}, u32[]{:S(2)}, u32[]{:S(2)}) %collective-permute-start.7) | collective-permute-done | bytes 131104 | tf_op jit(solution)/shard_map/ppermute | solution.py:16
  66.0 4.4 %collective-permute-start.9 = (f32[256,128]{1,0:T(8,128)S(1)}, f32[256,128]{1,0:T(8,128)S(1)}, u32[]{:S(2)}, u32[]{:S(2)}) collective-permute-start(f32[256,128]{1,0:T(8,128)S(1)} %add.4.own_ref), channel_id=1, source_target_pairs={{0,2},{1,3},{2,0},{3,1},{4,6},{5,7},{6,4},{7,5},{8,10},{9,11},{10,... | collective-permute-start | bytes 393224 | tf_op jit(solution)/shard_map/ppermute | solution.py:16
  70.5 1.9 %collective-permute-start.8 = (f32[256,128]{1,0:T(8,128)S(1)}, f32[256,128]{1,0:T(8,128)S(1)}, u32[]{:S(2)}, u32[]{:S(2)}) collective-permute-start(f32[256,128]{1,0:T(8,128)S(1)} %add.4.own_ref), channel_id=1, source_target_pairs={{0,16},{4,20},{8,24},{12,28},{16,32},{20,36},{24,40},{28,44},{32,4... | collective-permute-start | bytes 393224 | tf_op jit(solution)/shard_map/ppermute | solution.py:16
  72.4 0.8 collective-permute-done.9
  73.3 8.2 %all_gather.3.all_ref = f32[1024,128]{1,0:T(8,128)S(1)} all-gather(f32[512,128]{1,0:T(8,128)S(1)} %pad_maximum_fusion), channel_id=1, replica_groups={{0,1},{2,3},{4,5},{6,7},{8,9},{10,11},{12,13},{14,15},{16,17},{18,19},{..., dimensions={0}, use_global_device_ids=true | all-gather | bytes 786432 | tf_op jit(solution)/shard_map/all_gather | solution.py:213
  81.5 0.1 interact.1
  81.6 1.9 %collective-permute-start.10 = (f32[16,128]{1,0:T(8,128)S(1)}, f32[16,128]{1,0:T(8,128)S(1)}, u32[]{:S(2)}, u32[]{:S(2)}) collective-permute-start(f32[16,128]{1,0:T(8,128)S(1)} %interact.1), channel_id=1, source_target_pairs={{0,16},{4,20},{8,24},{12,28},{16,32},{20,36},{24,40},{28,44},{32,4... | collective-permute-start | bytes 24584 | tf_op jit(solution)/shard_map/ppermute | solution.py:16
  83.5 1.1 %collective-permute-done.8.pooled_ref = f32[256,128]{1,0:T(8,128)S(1)} collective-permute-done((f32[256,128]{1,0:T(8,128)S(1)}, f32[256,128]{1,0:T(8,128)S(1)}, u32[]{:S(2)}, u32[]{:S(2)}) %collective-permute-start.8) | collective-permute-done | bytes 131104 | tf_op jit(solution)/shard_map/ppermute | solution.py:16
  84.6 0.8 deliver.1
  85.4 7.5 %collective-permute-done.10 = f32[16,128]{1,0:T(8,128)S(1)} collective-permute-done((f32[16,128]{1,0:T(8,128)S(1)}, f32[16,128]{1,0:T(8,128)S(1)}, u32[]{:S(2)}, u32[]{:S(2)}) %collective-permute-start.10) | collective-permute-done | bytes 8224 | tf_op jit(solution)/shard_map/ppermute | solution.py:16
  92.9 0.6 copy.5
  (9 shorter events, 0.0 us)
Async XLA Ops:
  0.6 1.2 %copy-start = (f32[2,1024,128]{2,1,0:T(8,128)S(1)}, f32[2,1024,128]{2,1,0:T(8,128)}, u32[]{:S(2)}) copy-start(f32[2,1024,128]{2,1,0:T(8,128)} %table_ref.1) | copy-start | bytes 3145732
  1.9 0.8 copy-start.1
  3.5 29.5 %collective-permute-start.4 = (f32[320,128]{1,0:T(8,128)S(1)}, f32[320,128]{1,0:T(8,128)S(1)}, u32[]{:S(2)}, u32[]{:S(2)}) collective-permute-start(f32[320,128]{1,0:T(8,128)S(1)} %shard_map.45), channel_id=1, source_target_pairs={{0,508},{4,0},{8,4},{12,8},{16,12},{20,16},{24,20},{28,24},{32,28}... | collective-permute-start | bytes 491528 | tf_op jit(solution)/shard_map/ppermute | solution.py:16
  18.8 11.4 %collective-permute-start = (s32[64,128]{1,0:T(8,128)S(1)}, s32[64,128]{1,0:T(8,128)S(1)}, u32[]{:S(2)}, u32[]{:S(2)}) collective-permute-start(s32[64,128]{1,0:T(8,128)S(1)} %bitcast.8), channel_id=1, source_target_pairs={{0,484},{4,488},{8,492},{12,496},{16,500},{20,504},{24,508},{28,0}... | collective-permute-start | bytes 98312 | tf_op jit(solution)/shard_map/ppermute | solution.py:16
  31.1 10.4 %collective-permute-start.1 = (f32[320,128]{1,0:T(8,128)S(1)}, f32[320,128]{1,0:T(8,128)S(1)}, u32[]{:S(2)}, u32[]{:S(2)}) collective-permute-start(f32[320,128]{1,0:T(8,128)S(1)} %shard_map.41), channel_id=1, source_target_pairs={{0,4},{4,8},{8,12},{12,16},{16,20},{20,24},{24,28},{28,32},{32,36}... | collective-permute-start | bytes 491528 | tf_op jit(solution)/shard_map/ppermute | solution.py:16
  33.9 10.4 %collective-permute-start.5 = (f32[320,128]{1,0:T(8,128)S(1)}, f32[320,128]{1,0:T(8,128)S(1)}, u32[]{:S(2)}, u32[]{:S(2)}) collective-permute-start(f32[320,128]{1,0:T(8,128)S(1)} %shard_map.46), channel_id=1, source_target_pairs={{0,508},{4,0},{8,4},{12,8},{16,12},{20,16},{24,20},{28,24},{32,28}... | collective-permute-start | bytes 491528 | tf_op jit(solution)/shard_map/ppermute | solution.py:16
  42.4 10.4 %collective-permute-start.2 = (f32[320,128]{1,0:T(8,128)S(1)}, f32[320,128]{1,0:T(8,128)S(1)}, u32[]{:S(2)}, u32[]{:S(2)}) collective-permute-start(f32[320,128]{1,0:T(8,128)S(1)} %shard_map.42), channel_id=1, source_target_pairs={{0,4},{4,8},{8,12},{12,16},{16,20},{20,24},{24,28},{28,32},{32,36}... | collective-permute-start | bytes 491528 | tf_op jit(solution)/shard_map/ppermute | solution.py:16
  45.2 10.4 %collective-permute-start.6 = (f32[320,128]{1,0:T(8,128)S(1)}, f32[320,128]{1,0:T(8,128)S(1)}, u32[]{:S(2)}, u32[]{:S(2)}) collective-permute-start(f32[320,128]{1,0:T(8,128)S(1)} %shard_map.47), channel_id=1, source_target_pairs={{0,508},{4,0},{8,4},{12,8},{16,12},{20,16},{24,20},{28,24},{32,28}... | collective-permute-start | bytes 491528 | tf_op jit(solution)/shard_map/ppermute | solution.py:16
  53.7 10.4 %collective-permute-start.3 = (f32[320,128]{1,0:T(8,128)S(1)}, f32[320,128]{1,0:T(8,128)S(1)}, u32[]{:S(2)}, u32[]{:S(2)}) collective-permute-start(f32[320,128]{1,0:T(8,128)S(1)} %shard_map.43), channel_id=1, source_target_pairs={{0,4},{4,8},{8,12},{12,16},{16,20},{20,24},{24,28},{28,32},{32,36}... | collective-permute-start | bytes 491528 | tf_op jit(solution)/shard_map/ppermute | solution.py:16
  56.5 9.5 %collective-permute-start.7 = (f32[256,128]{1,0:T(8,128)S(1)}, f32[256,128]{1,0:T(8,128)S(1)}, u32[]{:S(2)}, u32[]{:S(2)}) collective-permute-start(f32[256,128]{1,0:T(8,128)S(1)} %shard_map.48), channel_id=1, source_target_pairs={{0,508},{4,0},{8,4},{12,8},{16,12},{20,16},{24,20},{28,24},{32,28}... | collective-permute-start | bytes 393224 | tf_op jit(solution)/shard_map/ppermute | solution.py:16
  66.0 7.2 %collective-permute-start.9 = (f32[256,128]{1,0:T(8,128)S(1)}, f32[256,128]{1,0:T(8,128)S(1)}, u32[]{:S(2)}, u32[]{:S(2)}) collective-permute-start(f32[256,128]{1,0:T(8,128)S(1)} %add.4.own_ref), channel_id=1, source_target_pairs={{0,2},{1,3},{2,0},{3,1},{4,6},{5,7},{6,4},{7,5},{8,10},{9,11},{10,... | collective-permute-start | bytes 393224 | tf_op jit(solution)/shard_map/ppermute | solution.py:16
  70.5 14.1 %collective-permute-start.8 = (f32[256,128]{1,0:T(8,128)S(1)}, f32[256,128]{1,0:T(8,128)S(1)}, u32[]{:S(2)}, u32[]{:S(2)}) collective-permute-start(f32[256,128]{1,0:T(8,128)S(1)} %add.4.own_ref), channel_id=1, source_target_pairs={{0,16},{4,20},{8,24},{12,28},{16,32},{20,36},{24,40},{28,44},{32,4... | collective-permute-start | bytes 393224 | tf_op jit(solution)/shard_map/ppermute | solution.py:16
  81.6 11.3 %collective-permute-start.10 = (f32[16,128]{1,0:T(8,128)S(1)}, f32[16,128]{1,0:T(8,128)S(1)}, u32[]{:S(2)}, u32[]{:S(2)}) collective-permute-start(f32[16,128]{1,0:T(8,128)S(1)} %interact.1), channel_id=1, source_target_pairs={{0,16},{4,20},{8,24},{12,28},{16,32},{20,36},{24,40},{28,44},{32,4... | collective-permute-start | bytes 24584 | tf_op jit(solution)/shard_map/ppermute | solution.py:16
